TPU v7x, 256 devices: a whole 4x4x8 slice. The times are simulated.
256 devices in a mesh: batch: 8 (over y, z_lo), space: 32 (over x, z_hi, core).
Axes of the slice: x: 4, y: 4, z: 8 (z_hi: 4, z_lo: 2; z = z_hi * 2 + z_lo), core: 2. Of those that a mesh axis runs over, the one named last changes fastest.
Arguments:
- features: bfloat16 [8, 160, 64, 512], P('batch', 'space'), may hold values from -6 to 6
- cotangent: bfloat16 [8, 160, 64, 512], P('batch', 'space'), may hold values from -6 to 6
- brick_count: int32 [8, 32], P('batch', 'space'), may hold values from 1 to 5, as said below
- destination: int32 [8, 160], P('batch', 'space'), may hold values from -1 to 63, as said below
- neighbours: int32 [8, 26, 160], P('batch', None, 'space'), may hold values from -1 to 4, as said below
- kernel_one: bfloat16 [64, 1728], replicated, may hold values from -0.15625 to 0.15625
- kernel_two: bfloat16 [64, 1728], replicated, may hold values from -0.15625 to 0.15625
Outputs:
- block_output: bfloat16 [8, 64, 64, 512], P('batch', 'space')
- grad_features: bfloat16 [8, 160, 64, 512], P('batch', 'space')
- grad_kernel_one: float32 [64, 1728], replicated
- grad_kernel_two: float32 [64, 1728], replicated
Inputs may be any that keep to these rules, and one draw needn't show every extreme that they name: `brick_count`: A volume holds at most 2 times the devices of space active bricks; some device holds exactly 5. `destination`: -1 exactly on inactive slots. A device's first min(count, 2) bricks go to its own work slots 0, 1, ... in order; its brick in slot 2 + k (k = 0, 1, 2) goes to a work slot of device (s + 1 + k) mod 32; every work slot receives at most one brick, every device receives at most one brick, and a receiving device's own bricks fill its slots below the received one. In every volume some device receives a brick in its work slot 1. `neighbours`: entries of inactive slots are -1; an entry is never the slot of an inactive brick. Bricks sit on a grid of 3 x 3 positions per device, and the offset along the first cell axis is the offset in the device index.
All inputs are finite; a program needn't handle non-finite values.
Results may differ from a plain program's by a relative error of at most 0.0041.
Values may be sent and summed in bfloat16 or wider, within the bound.
A program may use at most 128 MiB of HBM per device.

v0:
```python
import math

import jax
import jax.numpy as jnp
import numpy as np
from jax import lax
from jax.sharding import PartitionSpec as P

EDGE = 8
WORK_CAP = 2
CELLS = 512


def passed_along(x, axis, by):
    size = lax.axis_size(axis)
    pairs = [(i, i + by) for i in range(size) if 0 <= i + by < size]
    return lax.ppermute(x, axis, pairs)


def passed_along_2(x, axis, by):
    size = lax.axis_size(axis)
    return lax.ppermute(x, axis, [(i, (i + by) % size) for i in range(size)])


def cut_side(region, axis_number, offset, margin_width):
    if offset < 0:
        return lax.slice_in_dim(region, EDGE - margin_width, EDGE, axis=axis_number)
    if offset > 0:
        return lax.slice_in_dim(region, 0, margin_width, axis=axis_number)
    return region


def pick_rows(source, slot_index):
    present = slot_index >= 0
    chosen = jnp.take(source, jnp.maximum(slot_index, 0), axis=0)
    shaped = present.reshape((-1,) + (1,) * (source.ndim - 1))
    return jnp.where(shaped, chosen, jnp.zeros_like(chosen))


def assemble(home_block, from_lower, from_upper, link_table, margin_width):
    sources = (from_lower, home_block, from_upper)
    slab_list = []
    for along_first in (-1, 0, 1):
        row_list = []
        for along_second in (-1, 0, 1):
            pieces = []
            for along_third in (-1, 0, 1):
                number = 9 * (along_first + 1) + 3 * (along_second + 1) + (along_third + 1)
                if number == 13:
                    region = home_block
                else:
                    position = number if number < 13 else number - 1
                    region = pick_rows(sources[along_first + 1], link_table[position])
                region = cut_side(region, 3, along_second, margin_width)
                region = cut_side(region, 4, along_third, margin_width)
                pieces.append(region)
            row_list.append(jnp.concatenate(pieces, axis=4))
        slab_list.append(jnp.concatenate(row_list, axis=3))
    return jnp.concatenate(slab_list, axis=2)


def tap_offset(tap_number, side_len, negate):
    plane_tap, rest = divmod(tap_number, 9)
    row_tap, column = divmod(rest, 3)
    offset = (plane_tap - 1) * side_len * side_len + (row_tap - 1) * side_len + (column - 1)
    return -offset if negate else offset


def conv_region(flat_cells, kernel, side_len, negate):
    channels = flat_cells.shape[0]
    first_cell = side_len * side_len + side_len + 1
    stretch = side_len**3 - 2 * first_cell
    summed = jnp.zeros((kernel.shape[0], stretch), jnp.float32)
    for tap_number in range(27):
        offset = tap_offset(tap_number, side_len, negate)
        shifted = lax.slice_in_dim(
            flat_cells, first_cell + offset, first_cell + offset + stretch, axis=1
        )
        part_kernel = kernel[:, tap_number * channels : (tap_number + 1) * channels]
        summed = summed + jnp.dot(part_kernel, shifted, preferred_element_type=jnp.float32)
    spread = jnp.pad(summed, ((0, 0), (first_cell, first_cell)))
    volume = spread.reshape(-1, side_len, side_len, side_len)[:, 1:-1, 1:-1, 1:-1]
    return volume.reshape(volume.shape[0], -1)


def kernel_grad(flat_cells, inner_grad, side_len):
    channels = flat_cells.shape[0]
    margin_width = (side_len - EDGE) // 2
    first_cell = side_len * side_len + side_len + 1
    stretch = side_len**3 - 2 * first_cell
    grid = inner_grad.reshape(channels, EDGE, EDGE, EDGE)
    framed = jnp.pad(
        grid,
        (
            (0, 0),
            (margin_width, margin_width),
            (margin_width, margin_width),
            (margin_width, margin_width),
        ),
    )
    window = lax.slice_in_dim(
        framed.reshape(channels, -1), first_cell, first_cell + stretch, axis=1
    )
    parts = []
    for tap_number in range(27):
        offset = tap_offset(tap_number, side_len, False)
        shifted = lax.slice_in_dim(
            flat_cells, first_cell + offset, first_cell + offset + stretch, axis=1
        )
        parts.append(
            lax.dot_general(
                window, shifted, (((1,), (1,)), ((), ())), preferred_element_type=jnp.float32
            )
        )
    return jnp.concatenate(parts, axis=1)


def flip_kernel(kernel):
    channels = kernel.shape[0]
    return (
        kernel.reshape(channels, 27, channels).transpose(2, 1, 0).reshape(channels, 27 * channels)
    )


def crop_cells(flat_cells, side_len, margin_width):
    grid = flat_cells.reshape(-1, side_len, side_len, side_len)
    inner = grid[
        :,
        margin_width : side_len - margin_width,
        margin_width : side_len - margin_width,
        margin_width : side_len - margin_width,
    ]
    return inner.reshape(inner.shape[0], -1)


def cell_mask(presence):
    grid = presence.reshape(3, 3, 3)
    repeats = np.array([1, EDGE, 1])
    for axis_number in range(3):
        grid = jnp.repeat(grid, repeats, axis=axis_number, total_repeat_length=EDGE + 2)
    return grid.reshape(-1)


def brick_pass(padded_x, padded_dy, presence, kernels):
    kernel_one, kernel_two, flip_one, flip_two = kernels
    wide = EDGE + 4
    narrow = EDGE + 2
    channels = padded_x.shape[1]
    zero_grad = jnp.zeros((channels, 27 * channels), jnp.float32)

    def visit(carry, block_items):
        grad_one, grad_two = carry
        cells_x, cells_dy, present = block_items
        cycle_mask = cell_mask(present)
        first = conv_region(cells_x, kernel_one, wide, False)
        hidden = (jax.nn.silu(first) * cycle_mask).astype(jnp.bfloat16)
        second = conv_region(hidden, kernel_two, narrow, False)
        inner_x = crop_cells(cells_x, wide, 2)
        inner_dy = crop_cells(cells_dy, wide, 2)
        output = ((inner_x.astype(jnp.float32) + second) * present[13]).astype(jnp.bfloat16)
        grad_hidden = conv_region(cells_dy, flip_two, wide, True)
        sigma = jax.nn.sigmoid(first)
        grad_first = (grad_hidden * (sigma * (1.0 + first * (1.0 - sigma))) * cycle_mask).astype(
            jnp.bfloat16
        )
        back_input = conv_region(grad_first, flip_one, narrow, True).astype(jnp.bfloat16)
        grad_two = grad_two + kernel_grad(hidden, inner_dy, narrow)
        grad_one = grad_one + kernel_grad(cells_x, crop_cells(grad_first, narrow, 1), wide)
        return ((grad_one, grad_two), (output, back_input))

    return lax.scan(visit, (zero_grad, zero_grad), (padded_x, padded_dy, presence))


def place_arrival(own_rows, arrived_row, from_home, target_rows):
    remote = jnp.where(
        target_rows.reshape((-1,) + (1,) * (own_rows.ndim - 1)),
        arrived_row[None],
        jnp.zeros_like(own_rows),
    )
    shaped = from_home.reshape((-1,) + (1,) * (own_rows.ndim - 1))
    return jnp.where(shaped, own_rows, remote)


def shards(features, cotangent, brick_count, destination, neighbours, kernel_one, kernel_two):
    home_slots = features.shape[1]
    channels = features.shape[2]
    surplus_rows = home_slots - WORK_CAP
    devices = lax.axis_size("space")
    my_index = lax.axis_index("space")
    slot_ids = jnp.arange(home_slots, dtype=jnp.int32)
    work_ids = jnp.arange(WORK_CAP, dtype=jnp.int32)
    count_here = brick_count[0, 0]
    active = slot_ids < count_here
    keep = active[:, None, None]
    masked_x = jnp.where(keep, features[0], jnp.zeros_like(features[0]))
    masked_dy = jnp.where(keep, cotangent[0], jnp.zeros_like(cotangent[0]))
    cubes_x = masked_x.reshape(home_slots, channels, EDGE, EDGE, EDGE)
    cubes_dy = masked_dy.reshape(home_slots, channels, EDGE, EDGE, EDGE)
    lower_x, lower_dy = passed_along(
        (cubes_x[:, :, EDGE - 2 :], cubes_dy[:, :, EDGE - 2 :]), "space", 1
    )
    upper_x, upper_dy = passed_along((cubes_x[:, :, :2], cubes_dy[:, :, :2]), "space", -1)
    link_table = neighbours[0]
    padded_x = assemble(cubes_x, lower_x, upper_x, link_table, 2).reshape(home_slots, channels, -1)
    padded_dy = assemble(cubes_dy, lower_dy, upper_dy, link_table, 2).reshape(
        home_slots, channels, -1
    )
    linked = (link_table >= 0).astype(jnp.float32)
    centre = active.astype(jnp.float32)[None, :]
    presence = (jnp.concatenate([linked[:13], centre, linked[13:]], axis=0) * centre).T
    kernels = (kernel_one, kernel_two, flip_kernel(kernel_one), flip_kernel(kernel_two))
    arrival_live = jnp.zeros((devices,), jnp.bool_)
    arrival_slot = jnp.zeros((devices,), jnp.int32)
    for step in range(surplus_rows):
        row = WORK_CAP + step
        heard = passed_along_2(destination[0, row : row + 1], "space", step + 1)[0]
        source = (my_index - 1 - step) % devices
        hit = (heard >= 0) & (heard // WORK_CAP == my_index)
        arrival_live = arrival_live.at[source].set(hit)
        arrival_slot = arrival_slot.at[source].set(jnp.where(hit, heard - my_index * WORK_CAP, 0))
    from_home = work_ids < count_here
    remote_slot = jnp.sum(jnp.where(arrival_live, arrival_slot, 0))
    target_rows = jnp.any(arrival_live) & (work_ids == remote_slot)
    came_from = [arrival_live[(my_index - 1 - step) % devices] for step in range(surplus_rows)]
    presence_wire = presence.astype(jnp.bfloat16)
    got_x = jnp.zeros_like(padded_x[0])
    got_dy = jnp.zeros_like(padded_dy[0])
    got_presence = jnp.zeros_like(presence_wire[0])
    for step in range(surplus_rows):
        row = WORK_CAP + step
        live = active[row]
        moved_x, moved_dy, moved_presence = passed_along_2(
            (
                jnp.where(live, padded_x[row], jnp.zeros_like(padded_x[row])),
                jnp.where(live, padded_dy[row], jnp.zeros_like(padded_dy[row])),
                jnp.where(live, presence_wire[row], jnp.zeros_like(presence_wire[row])),
            ),
            "space",
            step + 1,
        )
        got_x = jnp.where(came_from[step], moved_x, got_x)
        got_dy = jnp.where(came_from[step], moved_dy, got_dy)
        got_presence = jnp.where(came_from[step], moved_presence, got_presence)
    work_x = place_arrival(padded_x[:WORK_CAP], got_x, from_home, target_rows)
    work_dy = place_arrival(padded_dy[:WORK_CAP], got_dy, from_home, target_rows)
    work_presence = place_arrival(
        presence[:WORK_CAP], got_presence.astype(jnp.float32), from_home, target_rows
    )
    grads, (work_out, work_back) = brick_pass(work_x, work_dy, work_presence, kernels)
    back_row = jnp.sum(
        jnp.where(target_rows[:, None, None], work_back.astype(jnp.float32), 0.0), axis=0
    ).astype(jnp.bfloat16)
    returned = []
    for step in range(surplus_rows):
        returned.append(
            passed_along_2(
                jnp.where(came_from[step], back_row, jnp.zeros_like(back_row)), "space", -(step + 1)
            )
        )
    back_home = jnp.concatenate([work_back, jnp.stack(returned)], axis=0)
    back_home = jnp.where(keep, back_home, jnp.zeros_like(back_home))
    grad_in = (masked_dy.astype(jnp.float32) + back_home.astype(jnp.float32)).astype(jnp.bfloat16)
    grad_one, grad_two = lax.psum((grads[0], grads[1]), ("batch", "space"))
    scale = 1.0 / math.sqrt(
        lax.axis_size("batch") * features.shape[0] * devices * home_slots * CELLS
    )
    return (work_out[None], grad_in[None], grad_one * scale, grad_two * scale)


def solution(mesh):
    return jax.shard_map(
        shards,
        mesh=mesh,
        in_specs=(
            P("batch", "space", None, None),
            P("batch", "space", None, None),
            P("batch", "space"),
            P("batch", "space"),
            P("batch", None, "space"),
            P(),
            P(),
        ),
        out_specs=(P("batch", "space", None, None), P("batch", "space", None, None), P(), P()),
        check_vma=False,
    )
```

profile of v0, /device:TPU:1, one launch (start us, length us, event | category | flops | bytes accessed | tf_op | source)
XLA Modules:
  0.0 848.0 jit_solution(5892501478910788538)
XLA Ops:
  8.6 4.4 collective-permute-start.2
  13.0 4.2 collective-permute-start.3
  22.1 2.3 collective-permute-start.9
  25.2 2.1 collective-permute-start.1
  30.2 2.4 compare_reduce_fusion.25
  34.4 1.9 maximum_reduce_fusion.25
  74.6 2.9 copy.61
  80.4 2.9 copy.65
  83.2 2.1 reshape.1011
  91.4 2.7 broadcast_select_fusion.10
  99.5 1.9 fusion.452
  101.5 4.5 collective-permute-start.8
  112.7 2.2 collective-permute-start.14
  126.6 5.2 collective-permute-start.15
  131.8 1.9 collective-permute-start
  133.7 1.9 fusion.449
  180.5 16.8 %maximum_maximum_fusion.1 = bf16[5,64,12,12,12]{1,4,3,2,0:T(8,128)(2,1)S(1)} fusion(bf16[5,64,2,2,2]{1,4,3,2,0:T(2,128)(2,1)} %get-tuple-element.689, bf16[5,64,2,2,8]{1,4,3,2,0:T(8,128)(2,1)} %get-tuple-element.687, bf16[5,64,2,2,2]{1,4,3,2,0:T(2,128)(2,1)} %get-tuple-element.685, bf16[5,64,2,8,2]{1,4,3,2,0:T(2,128)(2,1)} %get-tuple-element.683, ...), kind=kLoop, calls=%fused_computation.611 | loop fusion | flops 29859840 | bytes 2211840 | tf_op jit(solution)/shard_map/concatenate | solution.py:59
  197.6 4.8 maximum_select_fusion.2
  202.4 4.8 maximum_select_fusion.1
  207.4 5.0 maximum_select_fusion
  212.6 4.8 maximum_select_fusion.5
  217.4 4.8 maximum_select_fusion.4
  222.3 17.7 %maximum_maximum_fusion = bf16[5,64,12,12,12]{1,4,3,2,0:T(8,128)(2,1)} fusion(bf16[5,64,2,2,2]{1,4,3,2,0:T(2,128)(2,1)S(1)} %get-tuple-element.690, bf16[5,64,2,2,8]{1,4,3,2,0:T(8,128)(2,1)S(1)} %copy-done.41, bf16[5,64,2,2,2]{1,4,3,2,0:T(2,128)(2,1)S(1)} %get-tuple-element.686, bf16[5,64,2,8,2]{1,4,3,2,0:T(2,128)(2,1)S(1)} %copy-done.43, ...), kind=kLoop, calls=%fused_computation.610 | loop fusion | flops 29859840 | bytes 2211840 | tf_op jit(solution)/shard_map/concatenate | solution.py:59
  240.1 2.3 copy.63
  242.5 2.1 select_n.604
  244.5 2.6 collective-permute-start.10
  249.8 2.1 select_n.562
  251.9 5.5 collective-permute-start.5
  259.3 4.7 maximum_select_fusion.3
  267.7 4.0 collective-permute-start.7
  271.7 7.9 collective-permute-done.11
  279.6 11.9 %collective-permute-done.12 = bf16[64,1728]{0,1:T(8,128)(2,1)} collective-permute-done((bf16[64,1728]{0,1:T(8,128)(2,1)}, bf16[64,1728]{0,1:T(8,128)(2,1)}, u32[]{:S(2)}, u32[]{:S(2)}) %collective-permute-start.12) | collective-permute-done | bytes 221216 | tf_op jit(solution)/shard_map/ppermute | solution.py:22
  291.6 2.0 select_select_fusion
  293.6 11.0 %collective-permute-done.5 = bf16[64,1728]{0,1:T(8,128)(2,1)} collective-permute-done((bf16[64,1728]{0,1:T(8,128)(2,1)}, bf16[64,1728]{0,1:T(8,128)(2,1)}, u32[]{:S(2)}, u32[]{:S(2)}) %collective-permute-start.5) | collective-permute-done | bytes 221216 | tf_op jit(solution)/shard_map/ppermute | solution.py:22
  304.7 9.2 %collective-permute-done.6 = bf16[64,1728]{0,1:T(8,128)(2,1)S(1)} collective-permute-done((bf16[64,1728]{0,1:T(8,128)(2,1)}, bf16[64,1728]{0,1:T(8,128)(2,1)S(1)}, u32[]{:S(2)}, u32[]{:S(2)}) %collective-permute-start.6) | collective-permute-done | bytes 221216 | tf_op jit(solution)/shard_map/ppermute | solution.py:22
  313.9 7.2 collective-permute-done.7
  321.1 2.0 select_select_fusion.1
  323.1 2.4 broadcast_select_fusion
  326.7 231.7 %while.31 = (s32[]{:T(128)}, f32[64,1728]{1,0:T(8,128)}, f32[64,1728]{1,0:T(8,128)}, bf16[2,64,512]{2,1,0:T(8,128)(2,1)}, bf16[2,64,512]{1,2,0:T(8,128)(2,1)}, /...) while((s32[]{:T(128)}, f32[64,1728]{1,0:T(8,128)}, ...), condition=%wide.region_6.9_spmd.clone.clone, body=%wide.region_3.8_spmd.clone.clone.sunk | while | flops 1463709824 | bytes 167389072 | solution.py:171
  384.3 2.1 copy.91
  388.8 2.7 fusion.1201
  490.1 2.1 copy.91
  494.6 2.7 fusion.1201
  559.7 2.0 broadcast_select_fusion.16
  561.8 23.9 %collective-permute-start.17 = (bf16[64,512]{0,1:T(8,128)(2,1)S(1)}, bf16[64,512]{0,1:T(8,128)(2,1)S(1)}, u32[]{:S(2)}, u32[]{:S(2)}) collective-permute-start(bf16[64,512]{0,1:T(8,128)(2,1)S(1)} %get-tuple-element.630), channel_id=1, source_target_pairs={{0,30},{1,31},{2,0},{3,1},{4,2},{5,3},{6,4},{7,5},{8,6},{9,7},{10,... | collective-permute-start | bytes 196616 | tf_op jit(solution)/shard_map/ppermute | solution.py:22
  587.2 16.5 %collective-permute-done.17 = bf16[64,512]{0,1:T(8,128)(2,1)S(1)} collective-permute-done((bf16[64,512]{0,1:T(8,128)(2,1)S(1)}, bf16[64,512]{0,1:T(8,128)(2,1)S(1)}, u32[]{:S(2)}, u32[]{:S(2)}) %collective-permute-start.17) | collective-permute-done | bytes 65568 | tf_op jit(solution)/shard_map/ppermute | solution.py:22
  605.9 232.2 %all-reduce.9.cloned.1.call-done = (f32[64,1728]{1,0:T(8,128)}, f32[64,1728]{1,0:T(8,128)}) async-done(((f32[64,1728]{1,0:T(8,128)}, f32[64,1728]{1,0:T(8,128)}), (f32[64,1728]{1,0:T(8,128)}, f32[64,1728]{1,0:T(8,128)})) %all-reduce.9.cloned.1.call-update) | async-done | bytes 884752 | tf_op jit(solution)/shard_map/psum | solution.py:263
  838.0 1.9 broadcast_multiply_fusion.1
  (886 shorter events, 330.1 us)
Async XLA Ops:
  7.2 830.9 %all-reduce.9.cloned.1.call-start = ((), (), s32[]{:S(2)}) async-start(), calls=%async_computation | async-start | bytes 1835008 | tf_op jit(solution)/shard_map/psum | solution.py:263
  8.6 92.9 %collective-permute-start.2 = (s32[1]{0:T(128)}, s32[1]{0:T(128)}, u32[]{:S(2)}, u32[]{:S(2)}) collective-permute-start(s32[1]{0:T(128)} %bitcast.3), channel_id=1, source_target_pairs={{0,1},{1,2},{2,3},{3,4},{4,5},{5,6},{6,7},{7,8},{8,9},{9,10},{10,1... | collective-permute-start | bytes 20 | tf_op jit(solution)/shard_map/ppermute | solution.py:22
  13.0 95.9 %collective-permute-start.3 = (s32[1]{0:T(128)}, s32[1]{0:T(128)}, u32[]{:S(2)}, u32[]{:S(2)}) collective-permute-start(s32[1]{0:T(128)} %bitcast.7), channel_id=1, source_target_pairs={{0,2},{1,3},{2,4},{3,5},{4,6},{5,7},{6,8},{7,9},{8,10},{9,11},{10,... | collective-permute-start | bytes 20 | tf_op jit(solution)/shard_map/ppermute | solution.py:22
  17.2 95.6 %collective-permute-start.4 = (s32[1]{0:T(128)}, s32[1]{0:T(128)}, u32[]{:S(2)}, u32[]{:S(2)}) collective-permute-start(s32[1]{0:T(128)} %bitcast.11), channel_id=1, source_target_pairs={{0,3},{1,4},{2,5},{3,6},{4,7},{5,8},{6,9},{7,10},{8,11},{9,12},{10... | collective-permute-start | bytes 20 | tf_op jit(solution)/shard_map/ppermute | solution.py:22
  20.9 42.9 %copy-start.78 = (pred[5]{0:T(512)(128)(4,1)}, pred[5]{0:T(512)(128)(4,1)S(1)}, u32[]{:S(2)}) copy-start(pred[5]{0:T(512)(128)(4,1)S(1)} %get-tuple-element.702) | copy-start | bytes 19
  22.1 114.2 %collective-permute-start.9 = (bf16[5,64,2,8,8]{1,4,3,2,0:T(8,128)(2,1)}, bf16[5,64,2,8,8]{1,4,3,2,0:T(8,128)(2,1)S(1)}, u32[]{:S(2)}, u32[]{:S(2)}) collective-permute-start(bf16[5,64,2,8,8]{1,4,3,2,0:T(8,128)(2,1)} %get-tuple-element.626), channel_id=1, source_target_pairs={{1,0},{2,1},{3,2},{4,3},{5,4},{6,5},{7,6},{8,7},{9,8},{10,9},{11,1... | collective-permute-start | bytes 245768 | tf_op jit(solution)/shard_map/ppermute | solution.py:17
  25.2 111.8 %collective-permute-start.1 = (bf16[5,64,2,8,8]{1,4,3,2,0:T(8,128)(2,1)}, bf16[5,64,2,8,8]{1,4,3,2,0:T(8,128)(2,1)S(1)}, u32[]{:S(2)}, u32[]{:S(2)}) collective-permute-start(bf16[5,64,2,8,8]{1,4,3,2,0:T(8,128)(2,1)} %get-tuple-element.628), channel_id=1, source_target_pairs={{1,0},{2,1},{3,2},{4,3},{5,4},{6,5},{7,6},{8,7},{9,8},{10,9},{11,1... | collective-permute-start | bytes 245768 | tf_op jit(solution)/shard_map/ppermute | solution.py:17
  101.5 58.9 %collective-permute-start.8 = (bf16[5,64,2,8,8]{1,4,3,2,0:T(8,128)(2,1)}, bf16[5,64,2,8,8]{1,4,3,2,0:T(8,128)(2,1)S(1)}, u32[]{:S(2)}, u32[]{:S(2)}) collective-permute-start(bf16[5,64,2,8,8]{1,4,3,2,0:T(8,128)(2,1)} %get-tuple-element.625), channel_id=1, source_target_pairs={{0,1},{1,2},{2,3},{3,4},{4,5},{5,6},{6,7},{7,8},{8,9},{9,10},{10,1... | collective-permute-start | bytes 245768 | tf_op jit(solution)/shard_map/ppermute | solution.py:17
  108.8 17.8 %collective-permute-start.13 = (bf16[27]{0:T(256)(128)(2,1)S(1)}, bf16[27]{0:T(256)(128)(2,1)S(1)}, u32[]{:S(2)}, u32[]{:S(2)}) collective-permute-start(bf16[27]{0:T(256)(128)(2,1)S(1)} %get-tuple-element.636), channel_id=1, source_target_pairs={{0,3},{1,4},{2,5},{3,6},{4,7},{5,8},{6,9},{7,10},{8,11},{9,12},{10... | collective-permute-start | bytes 170 | tf_op jit(solution)/shard_map/ppermute | solution.py:22
  112.7 19.1 %collective-permute-start.14 = (bf16[27]{0:T(256)(128)(2,1)S(1)}, bf16[27]{0:T(256)(128)(2,1)S(1)}, u32[]{:S(2)}, u32[]{:S(2)}) collective-permute-start(bf16[27]{0:T(256)(128)(2,1)S(1)} %get-tuple-element.635), channel_id=1, source_target_pairs={{0,2},{1,3},{2,4},{3,5},{4,6},{5,7},{6,8},{7,9},{8,10},{9,11},{10,... | collective-permute-start | bytes 170 | tf_op jit(solution)/shard_map/ppermute | solution.py:22
  126.6 7.1 collective-permute-start.15
  131.8 29.2 %collective-permute-start = (bf16[5,64,2,8,8]{1,4,3,2,0:T(8,128)(2,1)}, bf16[5,64,2,8,8]{1,4,3,2,0:T(8,128)(2,1)S(1)}, u32[]{:S(2)}, u32[]{:S(2)}) collective-permute-start(bf16[5,64,2,8,8]{1,4,3,2,0:T(8,128)(2,1)} %get-tuple-element.627), channel_id=1, source_target_pairs={{0,1},{1,2},{2,3},{3,4},{4,5},{5,6},{6,7},{7,8},{8,9},{9,10},{10,1... | collective-permute-start | bytes 245768 | tf_op jit(solution)/shard_map/ppermute | solution.py:17
  180.3 42.0 %copy-start.73 = (bf16[5,64,2,2,2]{1,4,3,2,0:T(2,128)(2,1)}, bf16[5,64,2,2,2]{1,4,3,2,0:T(2,128)(2,1)S(1)}, u32[]{:S(2)}) copy-start(bf16[5,64,2,2,2]{1,4,3,2,0:T(2,128)(2,1)S(1)} %get-tuple-element.640) | copy-start | bytes 15364
  180.3 17.1 %copy-start.22 = (bf16[5,64,2,8,8]{1,4,3,2,0:T(8,128)(2,1)S(1)}, bf16[5,64,2,8,8]{1,4,3,2,0:T(8,128)(2,1)}, u32[]{:S(2)}) copy-start(bf16[5,64,2,8,8]{1,4,3,2,0:T(8,128)(2,1)} %get-tuple-element.681) | copy-start | bytes 245764
  180.3 17.1 %copy-start.25 = (bf16[5,64,2,8,8]{1,4,3,2,0:T(8,128)(2,1)S(1)}, bf16[5,64,2,8,8]{1,4,3,2,0:T(8,128)(2,1)}, u32[]{:S(2)}) copy-start(bf16[5,64,2,8,8]{1,4,3,2,0:T(8,128)(2,1)} %get-tuple-element.647) | copy-start | bytes 245764
  180.3 17.1 %copy-start.37 = (bf16[5,64,8,2,2]{1,4,3,2,0:T(2,128)(2,1)S(1)}, bf16[5,64,8,2,2]{1,4,3,2,0:T(2,128)(2,1)}, u32[]{:S(2)}) copy-start(bf16[5,64,8,2,2]{1,4,3,2,0:T(2,128)(2,1)} %get-tuple-element.671) | copy-start | bytes 61444
  180.4 17.1 %copy-start.38 = (bf16[5,64,8,2,2]{1,4,3,2,0:T(2,128)(2,1)S(1)}, bf16[5,64,8,2,2]{1,4,3,2,0:T(2,128)(2,1)}, u32[]{:S(2)}) copy-start(bf16[5,64,8,2,2]{1,4,3,2,0:T(2,128)(2,1)} %get-tuple-element.667) | copy-start | bytes 61444
  180.4 17.1 %copy-start.39 = (bf16[5,64,8,2,2]{1,4,3,2,0:T(2,128)(2,1)S(1)}, bf16[5,64,8,2,2]{1,4,3,2,0:T(2,128)(2,1)}, u32[]{:S(2)}) copy-start(bf16[5,64,8,2,2]{1,4,3,2,0:T(2,128)(2,1)} %get-tuple-element.661) | copy-start | bytes 61444
  180.4 17.1 %copy-start.40 = (bf16[5,64,8,2,2]{1,4,3,2,0:T(2,128)(2,1)S(1)}, bf16[5,64,8,2,2]{1,4,3,2,0:T(2,128)(2,1)}, u32[]{:S(2)}) copy-start(bf16[5,64,8,2,2]{1,4,3,2,0:T(2,128)(2,1)} %get-tuple-element.657) | copy-start | bytes 61444
  180.4 17.1 %copy-start.46 = (bf16[5,64,2,2,8]{1,4,3,2,0:T(8,128)(2,1)S(1)}, bf16[5,64,2,2,8]{1,4,3,2,0:T(8,128)(2,1)}, u32[]{:S(2)}) copy-start(bf16[5,64,2,2,8]{1,4,3,2,0:T(8,128)(2,1)} %get-tuple-element.687) | copy-start | bytes 61444
  180.4 17.1 %copy-start.48 = (bf16[5,64,2,8,2]{1,4,3,2,0:T(2,128)(2,1)S(1)}, bf16[5,64,2,8,2]{1,4,3,2,0:T(2,128)(2,1)}, u32[]{:S(2)}) copy-start(bf16[5,64,2,8,2]{1,4,3,2,0:T(2,128)(2,1)} %get-tuple-element.683) | copy-start | bytes 61444
  180.4 17.1 %copy-start.50 = (bf16[5,64,2,8,2]{1,4,3,2,0:T(2,128)(2,1)S(1)}, bf16[5,64,2,8,2]{1,4,3,2,0:T(2,128)(2,1)}, u32[]{:S(2)}) copy-start(bf16[5,64,2,8,2]{1,4,3,2,0:T(2,128)(2,1)} %get-tuple-element.679) | copy-start | bytes 61444
  180.4 17.1 %copy-start.52 = (bf16[5,64,2,2,8]{1,4,3,2,0:T(8,128)(2,1)S(1)}, bf16[5,64,2,2,8]{1,4,3,2,0:T(8,128)(2,1)}, u32[]{:S(2)}) copy-start(bf16[5,64,2,2,8]{1,4,3,2,0:T(8,128)(2,1)} %get-tuple-element.675) | copy-start | bytes 61444
  180.4 17.1 %copy-start.54 = (bf16[5,64,2,2,8]{1,4,3,2,0:T(8,128)(2,1)S(1)}, bf16[5,64,2,2,8]{1,4,3,2,0:T(8,128)(2,1)}, u32[]{:S(2)}) copy-start(bf16[5,64,2,2,8]{1,4,3,2,0:T(8,128)(2,1)} %get-tuple-element.653) | copy-start | bytes 61444
  180.4 17.1 %copy-start.55 = (bf16[5,64,2,8,2]{1,4,3,2,0:T(2,128)(2,1)S(1)}, bf16[5,64,2,8,2]{1,4,3,2,0:T(2,128)(2,1)}, u32[]{:S(2)}) copy-start(bf16[5,64,2,8,2]{1,4,3,2,0:T(2,128)(2,1)} %get-tuple-element.649) | copy-start | bytes 61444
  180.4 17.1 %copy-start.56 = (bf16[5,64,2,8,2]{1,4,3,2,0:T(2,128)(2,1)S(1)}, bf16[5,64,2,8,2]{1,4,3,2,0:T(2,128)(2,1)}, u32[]{:S(2)}) copy-start(bf16[5,64,2,8,2]{1,4,3,2,0:T(2,128)(2,1)} %get-tuple-element.645) | copy-start | bytes 61444
  180.5 17.1 %copy-start.57 = (bf16[5,64,2,2,8]{1,4,3,2,0:T(8,128)(2,1)S(1)}, bf16[5,64,2,2,8]{1,4,3,2,0:T(8,128)(2,1)}, u32[]{:S(2)}) copy-start(bf16[5,64,2,2,8]{1,4,3,2,0:T(8,128)(2,1)} %get-tuple-element.641) | copy-start | bytes 61444
  180.5 17.1 %copy-start.64 = (bf16[5,64,2,2,2]{1,4,3,2,0:T(2,128)(2,1)S(1)}, bf16[5,64,2,2,2]{1,4,3,2,0:T(2,128)(2,1)}, u32[]{:S(2)}) copy-start(bf16[5,64,2,2,2]{1,4,3,2,0:T(2,128)(2,1)} %get-tuple-element.689) | copy-start | bytes 15364
  180.5 17.1 %copy-start.67 = (bf16[5,64,2,2,2]{1,4,3,2,0:T(2,128)(2,1)S(1)}, bf16[5,64,2,2,2]{1,4,3,2,0:T(2,128)(2,1)}, u32[]{:S(2)}) copy-start(bf16[5,64,2,2,2]{1,4,3,2,0:T(2,128)(2,1)} %get-tuple-element.685) | copy-start | bytes 15364
  180.5 17.1 %copy-start.70 = (bf16[5,64,2,2,2]{1,4,3,2,0:T(2,128)(2,1)S(1)}, bf16[5,64,2,2,2]{1,4,3,2,0:T(2,128)(2,1)}, u32[]{:S(2)}) copy-start(bf16[5,64,2,2,2]{1,4,3,2,0:T(2,128)(2,1)} %get-tuple-element.677) | copy-start | bytes 15364
  180.5 17.1 %copy-start.72 = (bf16[5,64,2,2,2]{1,4,3,2,0:T(2,128)(2,1)S(1)}, bf16[5,64,2,2,2]{1,4,3,2,0:T(2,128)(2,1)}, u32[]{:S(2)}) copy-start(bf16[5,64,2,2,2]{1,4,3,2,0:T(2,128)(2,1)} %get-tuple-element.673) | copy-start | bytes 15364
  180.5 17.1 %copy-start.74 = (bf16[5,64,2,2,2]{1,4,3,2,0:T(2,128)(2,1)S(1)}, bf16[5,64,2,2,2]{1,4,3,2,0:T(2,128)(2,1)}, u32[]{:S(2)}) copy-start(bf16[5,64,2,2,2]{1,4,3,2,0:T(2,128)(2,1)} %get-tuple-element.655) | copy-start | bytes 15364
  244.5 23.1 %collective-permute-start.10 = (bf16[64,1728]{0,1:T(8,128)(2,1)}, bf16[64,1728]{0,1:T(8,128)(2,1)}, u32[]{:S(2)}, u32[]{:S(2)}) collective-permute-start(bf16[64,1728]{0,1:T(8,128)(2,1)} %select_n.604), channel_id=1, source_target_pairs={{0,3},{1,4},{2,5},{3,6},{4,7},{5,8},{6,9},{7,10},{8,11},{9,12},{10... | collective-permute-start | bytes 663560 | tf_op jit(solution)/shard_map/ppermute | solution.py:22
  248.1 31.5 %collective-permute-start.11 = (bf16[64,1728]{0,1:T(8,128)(2,1)}, bf16[64,1728]{0,1:T(8,128)(2,1)}, u32[]{:S(2)}, u32[]{:S(2)}) collective-permute-start(bf16[64,1728]{0,1:T(8,128)(2,1)} %select_n.606), channel_id=1, source_target_pairs={{0,2},{1,3},{2,4},{3,5},{4,6},{5,7},{6,8},{7,9},{8,10},{9,11},{10,... | collective-permute-start | bytes 663560 | tf_op jit(solution)/shard_map/ppermute | solution.py:22
  249.2 42.4 %collective-permute-start.12 = (bf16[64,1728]{0,1:T(8,128)(2,1)}, bf16[64,1728]{0,1:T(8,128)(2,1)}, u32[]{:S(2)}, u32[]{:S(2)}) collective-permute-start(bf16[64,1728]{0,1:T(8,128)(2,1)} %select_n.608), channel_id=1, source_target_pairs={{0,1},{1,2},{2,3},{3,4},{4,5},{5,6},{6,7},{7,8},{8,9},{9,10},{10,1... | collective-permute-start | bytes 663560 | tf_op jit(solution)/shard_map/ppermute | solution.py:22
  251.9 52.8 %collective-permute-start.5 = (bf16[64,1728]{0,1:T(8,128)(2,1)}, bf16[64,1728]{0,1:T(8,128)(2,1)}, u32[]{:S(2)}, u32[]{:S(2)}) collective-permute-start(bf16[64,1728]{0,1:T(8,128)(2,1)} %select_n.562), channel_id=1, source_target_pairs={{0,3},{1,4},{2,5},{3,6},{4,7},{5,8},{6,9},{7,10},{8,11},{9,12},{10... | collective-permute-start | bytes 663560 | tf_op jit(solution)/shard_map/ppermute | solution.py:22
  258.3 55.5 %collective-permute-start.6 = (bf16[64,1728]{0,1:T(8,128)(2,1)}, bf16[64,1728]{0,1:T(8,128)(2,1)S(1)}, u32[]{:S(2)}, u32[]{:S(2)}) collective-permute-start(bf16[64,1728]{0,1:T(8,128)(2,1)} %select_n.566), channel_id=1, source_target_pairs={{0,2},{1,3},{2,4},{3,5},{4,6},{5,7},{6,8},{7,9},{8,10},{9,11},{10,... | collective-permute-start | bytes 663560 | tf_op jit(solution)/shard_map/ppermute | solution.py:22
  267.7 53.4 %collective-permute-start.7 = (bf16[64,1728]{0,1:T(8,128)(2,1)S(1)}, bf16[64,1728]{0,1:T(8,128)(2,1)S(1)}, u32[]{:S(2)}, u32[]{:S(2)}) collective-permute-start(bf16[64,1728]{0,1:T(8,128)(2,1)S(1)} %copy-done.59), channel_id=1, source_target_pairs={{0,1},{1,2},{2,3},{3,4},{4,5},{5,6},{6,7},{7,8},{8,9},{9,10},{10,1... | collective-permute-start | bytes 663560 | tf_op jit(solution)/shard_map/ppermute | solution.py:22
  293.6 29.5 %copy-start.26 = (bf16[2,64,12,12,12]{1,0,4,3,2:T(2,128)(2,1)S(1)}, bf16[2,64,12,12,12]{1,0,4,3,2:T(2,128)(2,1)}, u32[]{:S(2)}) copy-start(bf16[2,64,12,12,12]{1,0,4,3,2:T(2,128)(2,1)} %copy.63) | copy-start | bytes 1327108
  293.6 29.5 %copy-start.82 = (pred[2]{0:T(512)(128)(4,1)S(1)}, pred[2]{0:T(512)(128)(4,1)}, u32[]{:S(2)}) copy-start(pred[2]{0:T(512)(128)(4,1)} %copy-done.81) | copy-start | bytes 10
  293.6 29.5 %copy-start.85 = (pred[2]{0:T(512)(128)(4,1)S(1)}, pred[2]{0:T(512)(128)(4,1)}, u32[]{:S(2)}) copy-start(pred[2]{0:T(512)(128)(4,1)} %copy-done.84) | copy-start | bytes 10
  326.7 231.7 %copy-start.83 = (pred[2]{0:T(512)(128)(4,1)S(1)}, pred[2]{0:T(512)(128)(4,1)}, u32[]{:S(2)}) copy-start(pred[2]{0:T(512)(128)(4,1)} %copy-done.81) | copy-start | bytes 10
  558.4 28.5 %copy-start.34 = (bf16[2,64,512]{1,2,0:T(8,128)(2,1)S(1)}, bf16[2,64,512]{1,2,0:T(8,128)(2,1)}, u32[]{:S(2)}) copy-start(bf16[2,64,512]{1,2,0:T(8,128)(2,1)} %get-tuple-element.914) | copy-start | bytes 393220
  559.6 45.3 %copy-start.31 = (bf16[1,5,64,512]{3,2,1,0:T(8,128)(2,1)S(1)}, bf16[1,5,64,512]{3,2,1,0:T(8,128)(2,1)}, u32[]{:S(2)}) copy-start(bf16[1,5,64,512]{3,2,1,0:T(8,128)(2,1)} %param.33) | copy-start | bytes 983044
  559.6 45.3 %copy-start.79 = (pred[5]{0:T(512)(128)(4,1)S(1)}, pred[5]{0:T(512)(128)(4,1)}, u32[]{:S(2)}) copy-start(pred[5]{0:T(512)(128)(4,1)} %copy-done.78) | copy-start | bytes 19
  561.7 25.4 %collective-permute-start.18 = (bf16[64,512]{0,1:T(8,128)(2,1)S(1)}, bf16[64,512]{0,1:T(8,128)(2,1)S(1)}, u32[]{:S(2)}, u32[]{:S(2)}) collective-permute-start(bf16[64,512]{0,1:T(8,128)(2,1)S(1)} %get-tuple-element.631), channel_id=1, source_target_pairs={{0,29},{1,30},{2,31},{3,0},{4,1},{5,2},{6,3},{7,4},{8,5},{9,6},{10... | collective-permute-start | bytes 196616 | tf_op jit(solution)/shard_map/ppermute | solution.py:22
  561.8 41.9 %collective-permute-start.17 = (bf16[64,512]{0,1:T(8,128)(2,1)S(1)}, bf16[64,512]{0,1:T(8,128)(2,1)S(1)}, u32[]{:S(2)}, u32[]{:S(2)}) collective-permute-start(bf16[64,512]{0,1:T(8,128)(2,1)S(1)} %get-tuple-element.630), channel_id=1, source_target_pairs={{0,30},{1,31},{2,0},{3,1},{4,2},{5,3},{6,4},{7,5},{8,6},{9,7},{10,... | collective-permute-start | bytes 196616 | tf_op jit(solution)/shard_map/ppermute | solution.py:22
  585.6 19.2 %collective-permute-start.16 = (bf16[64,512]{0,1:T(8,128)(2,1)S(1)}, bf16[64,512]{0,1:T(8,128)(2,1)S(1)}, u32[]{:S(2)}, u32[]{:S(2)}) collective-permute-start(bf16[64,512]{0,1:T(8,128)(2,1)S(1)} %get-tuple-element.629), channel_id=1, source_target_pairs={{0,31},{1,0},{2,1},{3,2},{4,3},{5,4},{6,5},{7,6},{8,7},{9,8},{10,9... | collective-permute-start | bytes 196616 | tf_op jit(solution)/shard_map/ppermute | solution.py:22
  (103 other events, 414.6 us)
Sparse Core Ops, SparseCore 0:
  559.8 278.2 all-reduce.8
where the time goes:
time: 857 us; the launch traced here: 848 us
  waiting for transfers between devices  297 us (35%)
  other arithmetic  154 us (18%)
  matrix products  154 us (18%)
  local copies, waits for them, and re-layouts  125 us (15%)
  starting transfers between devices  68.1 us (8%)
  between operations  27.9 us (3%)
  loops' own time  22.3 us (3%)
    psum x1, waiting for transfers between devices, shards(): grad_one, grad_two = lax.psum((grads[0], grads[1]), ('batch', 'space'))  232 us
    dot_general x216, matrix products, conv_region(): jnp.dot(part_kernel, shifted, preferred_element_type=jnp.float32)  96.9 us
    ppermute x15, waiting for transfers between devices, passed_along_2(): return lax.ppermute(x, axis, [(i, (i + by) % size) for i in range(size)])  64.9 us
    ppermute x15, starting transfers between devices, passed_along_2(): return lax.ppermute(x, axis, [(i, (i + by) % size) for i in range(size)])  57.2 us
    dot_general x108, matrix products, kernel_grad(): lax.dot_general(window, shifted, (((1,), (1,)), ((), ())), preferred_elem...  57.1 us
    gather x52, local copies, waits for them, and re-layouts, pick_rows(): chosen = jnp.take(source, jnp.maximum(slot_index, 0), axis=0)  47.2 us
    concatenate x2, other arithmetic, assemble(): return jnp.concatenate(slab_list, axis=2)  34.5 us
    select_n x26, other arithmetic, pick_rows(): return jnp.where(shaped, chosen, jnp.zeros_like(chosen))  32.7 us
  transfers between devices with their start and end apart: 20, of which 8 were waited for; matrix products, arithmetic and copies ran while one was open for 15% of the time, Pallas kernels for 0%

commit v1 on v0

v1 whole, which is shorter than its diff:
```python
import functools
import math

import jax
import jax.numpy as jnp
import numpy as np
from jax import lax
from jax.experimental import pallas as pl
from jax.experimental.pallas import tpu as pltpu
from jax.sharding import PartitionSpec as P

WORK_CAP = 2
HOME = 5
TILES = 4
SPAN = 6
C = 64
LANES = 128
TAPS = 27
MESH = pl.DeviceIdType.MESH
BF = jnp.bfloat16
F32 = jnp.float32


def shift_matrices():
    def column(q, r, blocks):
        m = np.zeros((len(blocks) * LANES, LANES), np.float32)
        for half in range(2):
            for b in range(8):
                for c in range(8):
                    bb, cc = b + q, c + r
                    kind = (2 if not 0 <= cc < 8 else 0) + (1 if not 0 <= bb < 8 else 0)
                    at = blocks.index(kind) * LANES + half * 64 + (bb % 8) * 8 + cc % 8
                    m[at, half * 64 + b * 8 + c] = 1.0
        return m

    s_q = np.concatenate([column(-1, 0, [1, 0]), column(1, 0, [1, 0])], axis=1)
    s_r = np.concatenate([column(0, -1, [0, 2]), column(0, 1, [0, 2])], axis=1)
    s_c = np.concatenate(
        [column(q, r, [1, 0, 2, 3]) for q, r in ((-1, -1), (-1, 1), (1, -1), (1, 1))], axis=1
    )
    return [jnp.asarray(m, BF) for m in (s_q, s_r, s_c)]


def lane_ids(rows):
    return lax.broadcasted_iota(jnp.int32, (rows, LANES), 1)


def swap_halves(v):
    return pltpu.roll(v, 64, 1)


def to_tiles(parts, lo):
    n0, n1, n2, n3 = parts
    return [
        jnp.where(lo, n0, swap_halves(n2)),
        jnp.where(lo, swap_halves(n0), n2),
        jnp.where(lo, n1, swap_halves(n3)),
        jnp.where(lo, swap_halves(n1), n3),
    ]


def from_tiles(tiles, lo):
    f0, f1, f2, f3 = tiles
    return [
        jnp.where(lo, f0, swap_halves(f1)),
        jnp.where(lo, f2, swap_halves(f3)),
        jnp.where(lo, swap_halves(f0), f1),
        jnp.where(lo, swap_halves(f2), f3),
    ]


def pieces(value):
    return [value[:, k * LANES : (k + 1) * LANES] for k in range(TILES)]


def offset_number(p, q, r):
    number = 9 * (p + 1) + 3 * (q + 1) + (r + 1)
    return number if number < 13 else number - 1


def build_columns(tiles_ref, e0_ref, e3_ref, low_ref, up_ref, links_ref, n, t_ref, d_ref, mats):
    s_q, s_r, s_c = mats
    lane = lane_ids(C)
    lo = lane < 64
    row = (lane % 64) // 8
    col = lane % 8

    def slot(p, q, r):
        if (p, q, r) == (0, 0, 0):
            return n
        found = links_ref[0, offset_number(p, q, r), n]
        return jnp.where(found < 0, HOME, found)

    slots = {
        (p, q, r): slot(p, q, r) for p in (-1, 0, 1) for q in (-1, 0, 1) for r in (-1, 0, 1)
    }

    def source(k, q, r):
        if k == 0:
            return jnp.where(lo, low_ref[slots[-1, q, r]], e3_ref[slots[0, q, r]])
        if k == SPAN - 1:
            return jnp.where(lo, e0_ref[slots[0, q, r]], up_ref[slots[1, q, r]])
        return tiles_ref[slots[0, q, r], k - 1]

    zero = jnp.zeros((C, LANES), BF)
    for k in range(SPAN):
        t1 = source(k, 0, 0)
        t2 = jnp.where(row == 0, source(k, 1, 0), jnp.where(row == 7, source(k, -1, 0), zero))
        t3 = jnp.where(col == 7, source(k, 0, -1), jnp.where(col == 0, source(k, 0, 1), zero))
        up_side = jnp.where(col == 7, source(k, -1, -1), jnp.where(col == 0, source(k, -1, 1), zero))
        down_side = jnp.where(col == 7, source(k, 1, -1), jnp.where(col == 0, source(k, 1, 1), zero))
        t4 = jnp.where(row == 7, up_side, jnp.where(row == 0, down_side, zero))
        rows = slice(k * C, (k + 1) * C)
        t_ref[rows, 0:LANES] = t2
        t_ref[rows, LANES : 2 * LANES] = t1
        t_ref[rows, 2 * LANES : 3 * LANES] = t3
        t_ref[rows, 3 * LANES : 4 * LANES] = t4
        d_ref[n, k, 4 * C : 5 * C, :] = t1

    def put(result, order):
        packed = result.astype(BF)
        for place, qr in enumerate(order):
            for k in range(SPAN):
                d_ref[n, k, qr * C : (qr + 1) * C, :] = packed[
                    k * C : (k + 1) * C, place * LANES : (place + 1) * LANES
                ]

    put(jnp.dot(t_ref[:, 0 : 2 * LANES], s_q[...], preferred_element_type=F32), (1, 7))
    put(jnp.dot(t_ref[:, LANES : 3 * LANES], s_r[...], preferred_element_type=F32), (3, 5))
    put(jnp.dot(t_ref[...], s_c[...], preferred_element_type=F32), (0, 2, 6, 8))


def halo_pack(tiles_a, tiles_b, lo):
    down = jnp.where(lo, swap_halves(tiles_a[3]), tiles_b[3])
    back = jnp.where(lo, tiles_b[0], swap_halves(tiles_a[0]))
    return down, back


def neighbours_ring(space):
    me = lax.axis_index("space")
    batch = lax.axis_index("batch")
    return (batch, lax.rem(me + 1, space)), (batch, lax.rem(me + space - 1, space))


def exchange(down_ref, back_ref, low_ref, up_ref, send_sem, recv_sem, space):
    following, previous = neighbours_ring(space)
    forward = pltpu.make_async_remote_copy(
        src_ref=down_ref, dst_ref=low_ref, send_sem=send_sem.at[0], recv_sem=recv_sem.at[0],
        device_id=following, device_id_type=MESH,
    )
    backward = pltpu.make_async_remote_copy(
        src_ref=back_ref, dst_ref=up_ref, send_sem=send_sem.at[1], recv_sem=recv_sem.at[1],
        device_id=previous, device_id_type=MESH,
    )
    return forward, backward


def greet(devices):
    barrier = pltpu.get_barrier_semaphore()
    for device in devices:
        pl.semaphore_signal(barrier, inc=1, device_id=device, device_id_type=MESH)
    return barrier


def first_halo_kernel(space, x_ref, dy_ref, low_ref, up_ref, down_buf, back_buf, send_sem, recv_sem):
    barrier = greet(neighbours_ring(space))
    lo = lane_ids(C) < 64
    for n in range(HOME):
        tx = to_tiles(pieces(x_ref[n]), lo)
        ty = to_tiles(pieces(dy_ref[n]), lo)
        down, back = halo_pack(tx, ty, lo)
        down_buf[n] = down
        back_buf[n] = back
    pl.semaphore_wait(barrier, 2)
    copies = exchange(down_buf, back_buf, low_ref, up_ref, send_sem, recv_sem, space)
    for copy in copies:
        copy.start()
    for copy in copies:
        copy.wait()


def second_halo_kernel(space, down_ref, back_ref, low_ref, up_ref, send_sem, recv_sem):
    barrier = greet(neighbours_ring(space))
    pl.semaphore_wait(barrier, 2)
    copies = exchange(down_ref, back_ref, low_ref, up_ref, send_sem, recv_sem, space)
    for copy in copies:
        copy.start()
    for copy in copies:
        copy.wait()


def unpack_halo(low_in, up_in, lows, ups):
    for n in range(HOME):
        lows[0][n] = low_in[n]
        lows[1][n] = swap_halves(low_in[n])
        ups[0][n] = up_in[n]
        ups[1][n] = swap_halves(up_in[n])
    zero = jnp.zeros((C, LANES), BF)
    for ref in (*lows, *ups):
        ref[HOME] = zero


def clear_last(tiles_ref, e0_ref, e3_ref):
    zero = jnp.zeros((C, LANES), BF)
    for j in range(TILES):
        tiles_ref[HOME, j] = zero
    e0_ref[HOME] = zero
    e3_ref[HOME] = zero


def first_kernel(
    x_ref, dy_ref, low_in, up_in, links_ref, count_ref, k1_ref, f2_ref, sq_ref, sr_ref, sc_ref,
    h_out, g_out, down_out, back_out, sums_out,
    xt, yt, ex0, ex3, ey0, ey3, lx, ly, ux, uy, t_buf, dx, dd, gpad, hpad, acc1, acc2,
):
    lane = lane_ids(C)
    lo = lane < 64
    mats = (sq_ref, sr_ref, sc_ref)
    unpack_halo(low_in, up_in, (lx, ly), (ux, uy))
    clear_last(xt, ex0, ex3)
    clear_last(yt, ey0, ey3)
    zero = jnp.zeros((C, LANES), BF)
    count = count_ref[0, 0]
    for n in range(HOME):
        live = jnp.where(n < count, 1.0, 0.0).astype(F32)
        for src, tiles_ref, e0, e3 in ((x_ref, xt, ex0, ex3), (dy_ref, yt, ey0, ey3)):
            masked = (src[n].astype(F32) * live).astype(BF)
            tiles = to_tiles(pieces(masked), lo)
            for j in range(TILES):
                tiles_ref[n, j] = tiles[j]
            e0[n] = swap_halves(tiles[0])
            e3[n] = swap_halves(tiles[3])
    for ref in (gpad, hpad):
        for j in (0, 1, 6, 7):
            ref[j] = zero
    acc1[...] = jnp.zeros_like(acc1)
    acc2[...] = jnp.zeros_like(acc2)

    def brick(n, _):
        build_columns(xt, ex0, ex3, lx, ux, links_ref, n, t_buf, dx, mats)
        build_columns(yt, ey0, ey3, ly, uy, links_ref, n, t_buf, dd, mats)
        hidden = []
        grads = []
        for j in range(TILES):
            pre = jnp.dot(
                k1_ref[...], dx[n, j : j + 3].reshape(TAPS * C, LANES), preferred_element_type=F32
            )
            grad_hidden = jnp.dot(
                f2_ref[...], dd[n, j : j + 3].reshape(TAPS * C, LANES), preferred_element_type=F32
            )
            sigma = 1.0 / (1.0 + jnp.exp(-pre))
            hid = (pre * sigma).astype(BF)
            gpre = (grad_hidden * (sigma * (1.0 + pre * (1.0 - sigma)))).astype(BF)
            h_out[n, j] = hid
            g_out[n, j] = gpre
            hpad[j + 2] = hid
            gpad[j + 2] = gpre
            hidden.append(hid)
            grads.append(gpre)
        down, back = halo_pack(hidden, grads, lo)
        down_out[n] = down
        back_out[n] = back
        for acc, cols, pad, flip in ((acc1, dx, gpad, False), (acc2, dd, hpad, True)):
            total = acc[...]
            for k in (0, 2, 4):
                left = jnp.concatenate([cols[n, k], cols[n, k + 1]], axis=1)

                def right(at):
                    if flip:
                        return jnp.concatenate([pad[at + 1], pad[at], zero, pad[at + 2]], axis=0)
                    return jnp.concatenate([pad[at], pad[at + 1], pad[at + 2], zero], axis=0)

                both = jnp.concatenate([right(k), right(k + 1)], axis=1)
                total = total + lax.dot_general(
                    left, both, (((1,), (1,)), ((), ())), preferred_element_type=F32
                )
            acc[...] = total
        return 0

    lax.fori_loop(0, HOME, brick, 0)
    wide = lane_ids(9 * C) < 64
    first_a, first_b = acc1[:, 0:LANES], acc1[:, LANES : 2 * LANES]
    second_a, second_b = acc2[:, 0:LANES], acc2[:, LANES : 2 * LANES]
    sums_out[0 : 9 * C, :] = jnp.where(wide, first_b, second_b).astype(BF)
    sums_out[9 * C : 18 * C, :] = jnp.where(wide, second_a, first_a).astype(BF)
    sums_out[18 * C : 27 * C, :] = jnp.where(wide, first_a, second_a).astype(BF)
    sums_out[27 * C : 2048, :] = jnp.zeros((2048 - 27 * C, LANES), BF)


def second_kernel(
    x_ref, dy_ref, h_ref, g_ref, low_in, up_in, links_ref, count_ref, k2_ref, f1_ref,
    sq_ref, sr_ref, sc_ref, out_ref, grad_ref,
    ht, gt, eh0, eh3, eg0, eg3, lh, lg, uh, ug, t_buf, dh, dg,
):
    lane = lane_ids(C)
    lo = lane < 64
    mats = (sq_ref, sr_ref, sc_ref)
    unpack_halo(low_in, up_in, (lh, lg), (uh, ug))
    clear_last(ht, eh0, eh3)
    clear_last(gt, eg0, eg3)
    count = count_ref[0, 0]
    for n in range(HOME):
        for src, tiles_ref, e0, e3 in ((h_ref, ht, eh0, eh3), (g_ref, gt, eg0, eg3)):
            for j in range(TILES):
                tiles_ref[n, j] = src[n, j]
            e0[n] = swap_halves(src[n, 0])
            e3[n] = swap_halves(src[n, 3])

    def brick(n, _):
        build_columns(ht, eh0, eh3, lh, uh, links_ref, n, t_buf, dh, mats)
        build_columns(gt, eg0, eg3, lg, ug, links_ref, n, t_buf, dg, mats)
        mixed = []
        backs = []
        for j in range(TILES):
            mixed.append(jnp.dot(
                k2_ref[...], dh[n, j : j + 3].reshape(TAPS * C, LANES), preferred_element_type=F32
            ))
            backs.append(jnp.dot(
                f1_ref[...], dg[n, j : j + 3].reshape(TAPS * C, LANES), preferred_element_type=F32
            ))
        live = jnp.where(n < count, 1.0, 0.0).astype(F32)
        for k, (m, b) in enumerate(zip(from_tiles(mixed, lo), from_tiles(backs, lo))):
            lanes = slice(k * LANES, (k + 1) * LANES)
            out_ref[n, :, lanes] = ((x_ref[n, :, lanes].astype(F32) + m) * live).astype(BF)
            term = b.astype(BF).astype(F32)
            grad_ref[n, :, lanes] = ((dy_ref[n, :, lanes].astype(F32) + term) * live).astype(BF)
        return 0

    lax.fori_loop(0, HOME, brick, 0)


def finish_kernel(
    space, scale, s_ref, ob_ref, work_ref, one_ref, two_ref,
    r1, p2, r2, q_buf, a2, chunk, a1, arrived, total,
    s1s, s1r, s2s, s2r, g2s, g2r, g1s, g1r, obs, obr,
):
    batch = lax.axis_index("batch")
    at = lax.axis_index("space")
    y, z_lo = batch // 2, lax.rem(batch, 2)
    x, inner = at // 8, lax.rem(at, 8)
    g = x * 4 + y
    h = z_lo * 8 + inner

    def plane_peer(number):
        return (lax.rem(number, 4) * 2 + z_lo, (number // 4) * 8 + inner)

    def column_peer(number):
        return (y * 2 + number // 8, x * 8 + lax.rem(number, 8))

    def ring(step):
        return (batch, lax.rem(at + space + step, space))

    plane = [plane_peer(lax.rem(g + d, 16)) for d in range(1, 16)]
    column = [column_peer(lax.rem(h + d, 16)) for d in range(1, 16)]
    barrier = greet(plane + column + [ring(-1), ring(-2), ring(-3)])
    pl.semaphore_wait(barrier, 33)

    def start(src, dst, sends, recvs, number, device):
        copy = pltpu.make_async_remote_copy(
            src_ref=src, dst_ref=dst, send_sem=sends.at[number], recv_sem=recvs.at[number],
            device_id=device, device_id_type=MESH,
        )
        copy.start()
        return copy

    scatter = [
        start(s_ref.at[lax.rem(g + d, 16)], r1.at[d - 1], s1s, s1r, d - 1, plane[d - 1])
        for d in range(1, 16)
    ]
    bricks = [
        start(ob_ref.at[WORK_CAP + k], arrived.at[k], obs, obr, k, ring(k + 1)) for k in range(3)
    ]
    acc = s_ref[g].astype(F32)
    for d in range(15):
        scatter[d].wait_recv()
        acc = acc + r1[d].astype(F32)
    p2[...] = acc.reshape(16, 8, LANES)
    column_scatter = [
        start(p2.at[lax.rem(h + d, 16)], r2.at[d - 1], s2s, s2r, d - 1, column[d - 1])
        for d in range(1, 16)
    ]
    piece = p2[h]
    for d in range(15):
        column_scatter[d].wait_recv()
        piece = piece + r2[d]
    q_buf[...] = piece
    a2[h] = piece
    column_gather = [
        start(q_buf, a2.at[h], g2s, g2r, d - 1, column[d - 1]) for d in range(1, 16)
    ]
    for d in range(15):
        column_gather[d].wait_recv()
    whole = a2[...].reshape(LANES, LANES).astype(BF)
    chunk[...] = whole
    a1[g] = whole
    gather = [start(chunk, a1.at[g], g1s, g1r, d - 1, plane[d - 1]) for d in range(1, 16)]
    for k in range(3):
        bricks[k].wait_recv()
    work_ref[0] = ob_ref[0]
    extra = arrived[0].astype(F32) + arrived[1].astype(F32) + arrived[2].astype(F32)
    work_ref[1] = (ob_ref[1].astype(F32) + extra).astype(BF)
    for d in range(15):
        gather[d].wait_recv()
    total[...] = a1[...].reshape(2048, LANES).astype(F32) * scale
    lo = lane_ids(C) < 64

    def block(tap):
        return total[tap * C : (tap + 1) * C, :]

    def swapped(tap):
        return 9 <= tap < 18

    def first_block(tap, low):
        value = block(tap)
        return value if swapped(tap) != low else swap_halves(value)

    def second_block(tap, low):
        value = block(TAPS - 1 - tap)
        return value if swapped(tap) == low else swap_halves(value)

    for tile in range(14):
        tap = 2 * tile
        here = first_block(tap, True)
        there = second_block(tap, True)
        if tap + 1 < TAPS:
            pair = jnp.concatenate([here, first_block(tap + 1, True)], axis=0)
            one_ref[:, tile * LANES : (tile + 1) * LANES] = pair.T[0:C, :]
            two_ref[:, tile * LANES : (tile + 1) * LANES] = jnp.where(
                lo, there, second_block(tap + 1, False)
            )
        else:
            pair = jnp.concatenate([here, here], axis=0)
            one_ref[:, tile * LANES : tile * LANES + C] = pair.T[0:C, 0:C]
            two_ref[:, tile * LANES : tile * LANES + C] = there[:, 0:C]
    for copy in (*scatter, *column_scatter, *column_gather, *gather, *bricks):
        copy.wait_send()


def vmem():
    return pl.BlockSpec(memory_space=pltpu.VMEM)


def smem():
    return pl.BlockSpec(memory_space=pltpu.SMEM)


def bf_scratch(*shape):
    return pltpu.VMEM(shape, BF)


def flip_kernel(kernel):
    channels = kernel.shape[0]
    taps = kernel.reshape(channels, TAPS, channels)[:, ::-1, :]
    return taps.transpose(2, 1, 0).reshape(channels, TAPS * channels)


def field_scratch():
    tiles = [bf_scratch(HOME + 1, TILES, C, LANES)] * 2
    rows = [bf_scratch(HOME + 1, C, LANES)] * 8
    columns = [bf_scratch(SPAN * C, 4 * LANES)] + [bf_scratch(HOME, SPAN, 9 * C, LANES)] * 2
    return tiles + rows + columns


def halo_call(kernel, number, extra, args):
    return pl.pallas_call(
        kernel,
        out_shape=[jax.ShapeDtypeStruct((HOME, C, LANES), BF)] * 2,
        in_specs=[vmem()] * 2,
        out_specs=[vmem()] * 2,
        scratch_shapes=[*extra, pltpu.SemaphoreType.DMA((2,)), pltpu.SemaphoreType.DMA((2,))],
        compiler_params=pltpu.CompilerParams(collective_id=number, has_side_effects=True),
    )(*args)


def shards(space, groups, features, cotangent, brick_count, destination, neighbours, kernel_one, kernel_two):
    x = features[0]
    dy = cotangent[0]
    mats = shift_matrices()
    halo = bf_scratch(HOME, C, LANES)
    low, up = halo_call(functools.partial(first_halo_kernel, space), 0, [halo, halo], (x, dy))
    tile_shape = jax.ShapeDtypeStruct((HOME, TILES, C, LANES), BF)
    halo_shape = jax.ShapeDtypeStruct((HOME, C, LANES), BF)
    local = pltpu.CompilerParams(vmem_limit_bytes=60 * 1024 * 1024)
    hidden, gpre, down, back, sums = pl.pallas_call(
        first_kernel,
        out_shape=[
            tile_shape, tile_shape, halo_shape, halo_shape,
            jax.ShapeDtypeStruct((2048, LANES), BF),
        ],
        in_specs=[vmem()] * 4 + [smem()] * 2 + [vmem()] * 5,
        out_specs=[vmem()] * 5,
        scratch_shapes=field_scratch()
        + [bf_scratch(8, C, LANES)] * 2
        + [pltpu.VMEM((9 * C, 2 * LANES), F32)] * 2,
        compiler_params=local,
    )(x, dy, low, up, neighbours, brick_count, kernel_one, flip_kernel(kernel_two), *mats)
    low, up = halo_call(functools.partial(second_halo_kernel, space), 1, [], (down, back))
    bricks_shape = jax.ShapeDtypeStruct((HOME, C, TILES * LANES), BF)
    out, grad_in = pl.pallas_call(
        second_kernel,
        out_shape=[bricks_shape, bricks_shape],
        in_specs=[vmem()] * 6 + [smem()] * 2 + [vmem()] * 5,
        out_specs=[vmem()] * 2,
        scratch_shapes=field_scratch(),
        compiler_params=local,
    )(x, dy, hidden, gpre, low, up, neighbours, brick_count, kernel_two, flip_kernel(kernel_one), *mats)
    scale = 1.0 / math.sqrt(groups * space * HOME * TILES * LANES)
    grad_shape = jax.ShapeDtypeStruct((C, TAPS * C), F32)
    dma = pltpu.SemaphoreType.DMA
    work, grad_one, grad_two = pl.pallas_call(
        functools.partial(finish_kernel, space, scale),
        out_shape=[
            jax.ShapeDtypeStruct((WORK_CAP, C, TILES * LANES), BF), grad_shape, grad_shape,
        ],
        in_specs=[vmem()] * 2,
        out_specs=[vmem()] * 3,
        scratch_shapes=[
            bf_scratch(15, LANES, LANES),
            pltpu.VMEM((16, 8, LANES), F32),
            pltpu.VMEM((15, 8, LANES), F32),
            pltpu.VMEM((8, LANES), F32),
            pltpu.VMEM((16, 8, LANES), F32),
            bf_scratch(LANES, LANES),
            bf_scratch(16, LANES, LANES),
            bf_scratch(3, C, TILES * LANES),
            pltpu.VMEM((2048, LANES), F32),
        ]
        + [dma((15,))] * 8
        + [dma((3,))] * 2,
        compiler_params=pltpu.CompilerParams(collective_id=2, has_side_effects=True),
    )(sums.reshape(16, LANES, LANES), out)
    return work[None], grad_in[None], grad_one, grad_two


def solution(mesh):
    return jax.shard_map(
        functools.partial(shards, mesh.shape["space"], mesh.shape["batch"]),
        mesh=mesh,
        in_specs=(
            P("batch", "space", None, None),
            P("batch", "space", None, None),
            P("batch", "space"),
            P("batch", "space"),
            P("batch", None, "space"),
            P(),
            P(),
        ),
        out_specs=(P("batch", "space", None, None), P("batch", "space", None, None), P(), P()),
        check_vma=False,
    )
```

time: 857 us -> 99.7 us (0.12)
  waiting for transfers between devices: 297 us -> 0 us
  matrix products: 154 us -> 0 us
  other arithmetic: 154 us -> 0 us
  local copies, waits for them, and re-layouts: 125 us -> 11.3 us
  Pallas kernels: 0 us -> 85.3 us
  starting transfers between devices: 68.1 us -> 0 us
  between operations: 27.9 us -> 1.39 us
  loops' own time: 22.3 us -> 0 us
    psum x1 -> x0, waiting for transfers between devices: 232 us -> none  [shards(): grad_one, grad_two = lax.psum((grads[0], grads[1]), ('batch', 'space'))]
    dot_general x324 -> x0, matrix products: 154 us -> none  [the longest x216 96.9 us: conv_region(): jnp.dot(part_kernel, shifted, preferred_element_type=jnp.float32)]
    pallas_call x0 -> x5, Pallas kernels: none -> 85.3 us  [the longest x1 38.4 us: shards(): pl.pallas_call(functools.partial(finish_kernel, space, scale), out_shape=...]
    select_n x53 -> x0, other arithmetic: 73 us -> none  [the longest x26 32.7 us: pick_rows(): return jnp.where(shaped, chosen, jnp.zeros_like(chosen))]
    ppermute x19 -> x0, starting transfers between devices: 68.1 us -> none  [the longest x15 57.2 us: passed_along_2(): return lax.ppermute(x, axis, [(i, (i + by) % size) for i in range(size)])]
    ppermute x19 -> x0, waiting for transfers between devices: 64.9 us -> none  [the longest x15 64.9 us: passed_along_2(): return lax.ppermute(x, axis, [(i, (i + by) % size) for i in range(size)])]
    gather x58 -> x0, local copies, waits for them, and re-layouts: 50.6 us -> none  [the longest x52 47.2 us: pick_rows(): chosen = jnp.take(source, jnp.maximum(slot_index, 0), axis=0)]
    concatenate x2 -> x0, other arithmetic: 34.5 us -> none  [assemble(): return jnp.concatenate(slab_list, axis=2)]
  transfers between devices with their start and end apart: 20 -> 0, of which waited for: 8 -> 0; matrix products, arithmetic and copies ran while one was open for 15% -> 0% of each run, Pallas kernels for 0% -> 0%
where the time goes in v1:
time: 99.7 us; the launch traced here: 98 us
  Pallas kernels  85.3 us (86%)
  local copies, waits for them, and re-layouts  11.3 us (11%)
  between operations  1.39 us (1%)
    pallas_call x1, Pallas kernels, shards(): pl.pallas_call(functools.partial(finish_kernel, space, scale), out_shape=...  38.4 us
    pallas_call x2, Pallas kernels, halo_call(): pl.pallas_call(kernel, out_shape=[jax.ShapeDtypeStruct((HOME, C, LANES),...  22.6 us
    pallas_call x1, Pallas kernels, shards(): pl.pallas_call(first_kernel, out_shape=[tile_shape, tile_shape, halo_shap...  13.6 us
    pallas_call x1, Pallas kernels, shards(): pl.pallas_call(second_kernel, out_shape=[bricks_shape, bricks_shape], in_...  10.8 us
    unnamed x12, local copies, waits for them, and re-layouts  4.93 us
    reshape x2, local copies, waits for them, and re-layouts, flip_kernel(): return taps.transpose(2, 1, 0).reshape(channels, TAPS * channels)  2.21 us
    transpose x2, local copies, waits for them, and re-layouts, flip_kernel(): return taps.transpose(2, 1, 0).reshape(channels, TAPS * channels)  2.15 us

profile of v1, /device:TPU:1, one launch (start us, length us, event | category | flops | bytes accessed | tf_op | source)
XLA Modules:
  0.0 98.0 jit_solution(13022061560555726375)
XLA Ops:
  0.6 0.0 copy-start.3
  1.3 0.0 copy-done.3
  1.3 0.7 copy.18.links_ref
  2.0 0.0 copy-start
  2.0 12.0 %shard_map.120 = (bf16[5,64,128]{2,1,0:T(8,128)(2,1)}, bf16[5,64,128]{2,1,0:T(8,128)(2,1)}) custom-call(bf16[5,64,512]{2,1,0:T(8,128)(2,1)} %bitcast.7, bf16[5,64,512]{2,1,0:T(8,128)(2,1)} %bitcast.10), custom_call_target="tpu_custom_call" | custom-call | tf_op jit(solution)/shard_map/pallas_call | solution.py:465
  14.0 0.0 copy-done
  14.0 0.5 reshape.26
  14.5 0.5 rev.7
  15.1 1.1 %copy.19 = bf16[64,27,64]{2,1,0:T(8,128)(2,1)S(1)} copy(bf16[64,27,64]{0,1,2:T(8,128)(2,1)S(1)} %bitcast.13) | data formatting | bytes 442368 | tf_op jit(solution)/shard_map/transpose | solution.py:454
  16.2 0.0 copy-start.1
  16.2 1.1 %reshape.27.f1_ref = bf16[64,1728]{1,0:T(8,128)(2,1)} reshape(bf16[64,27,64]{2,1,0:T(8,128)(2,1)S(1)} %copy.19) | data formatting | bytes 442368 | tf_op jit(solution)/shard_map/reshape | solution.py:454
  17.3 0.0 copy-done.1
  17.3 0.5 reshape.23
  17.8 0.5 rev.6
  18.3 1.1 %copy.17 = bf16[64,27,64]{2,1,0:T(8,128)(2,1)S(1)} copy(bf16[64,27,64]{0,1,2:T(8,128)(2,1)S(1)} %bitcast.14) | data formatting | bytes 442368 | tf_op jit(solution)/shard_map/transpose | solution.py:454
  19.4 1.1 %reshape.24.f2_ref = bf16[64,1728]{1,0:T(8,128)(2,1)} reshape(bf16[64,27,64]{2,1,0:T(8,128)(2,1)S(1)} %copy.17) | data formatting | bytes 442368 | tf_op jit(solution)/shard_map/reshape | solution.py:454
  20.5 13.6 %shard_map.121 = (bf16[5,4,64,128]{3,2,1,0:T(8,128)(2,1)}, bf16[5,4,64,128]{3,2,1,0:T(8,128)(2,1)}, bf16[5,64,128]{2,1,0:T(8,128)(2,1)}, bf16[5,64,128]{2,1,0:T(8,128)(2,1)}, bf16[2048,128]{1,0:T(8,128)(2,1)}) custom-call(bf16[5,64,512]{2,1,0:T(8,128)(2,1)} %bitcast.8, bf16[5,64,512]{2,1,0:T(8,128)(2,1)} %bitcast.11, ...), custom_call_target="tpu_custom_call" | custom-call | tf_op jit(solution)/shard_map/pallas_call | solution.py:484
  34.1 10.6 %shard_map.122 = (bf16[5,64,128]{2,1,0:T(8,128)(2,1)}, bf16[5,64,128]{2,1,0:T(8,128)(2,1)}) custom-call(bf16[5,64,128]{2,1,0:T(8,128)(2,1)} %get-tuple-element.23.down_ref, bf16[5,64,128]{2,1,0:T(8,128)(2,1)} %get-tuple-element.24.back_ref), custom_call_target="tpu_custom_call" | custom-call | tf_op jit(solution)/shard_map/pallas_call | solution.py:465
  44.7 10.8 %shard_map.123 = (bf16[5,64,512]{2,1,0:T(8,128)(2,1)}, bf16[5,64,512]{2,1,0:T(8,128)(2,1)}) custom-call(bf16[5,64,512]{2,1,0:T(8,128)(2,1)} %bitcast.9, bf16[5,64,512]{2,1,0:T(8,128)(2,1)} %bitcast.12, bf16[5,4,64,128]{3,2,1,0:T(8,128)(2,1)} %get-tuple-element.21.h_ref, bf16[5,4,64,128]{3,2,1,0:T(8,128)(2,1)} %get-tuple-element.22.g_ref, ...), custom_call_target="tpu_custom_call" | custom-call | tf_op jit(solution)/shard_map/pallas_call | solution.py:499
  55.5 38.4 %shard_map.124 = (bf16[2,64,512]{2,1,0:T(8,128)(2,1)}, f32[64,1728]{1,0:T(8,128)}, f32[64,1728]{1,0:T(8,128)}) custom-call(bf16[16,128,128]{2,1,0:T(8,128)(2,1)} %bitcast.15, bf16[5,64,512]{2,1,0:T(8,128)(2,1)} %get-tuple-element.27.ob_ref), custom_call_target="tpu_custom_call" | custom-call | tf_op jit(solution)/shard_map/pallas_call | solution.py:510
  93.8 1.6 %copy.25 = bf16[1,2,64,512]{3,2,1,0:T(8,128)(2,1)} copy(bf16[1,2,64,512]{3,2,1,0:T(8,128)(2,1)} %bitcast.16) | data formatting | bytes 262144
  95.4 0.0 copy-start.2
  95.4 1.9 %copy.26 = f32[64,1728]{1,0:T(8,128)} copy(f32[64,1728]{1,0:T(8,128)} %get-tuple-element.38) | data formatting | bytes 884736
  97.3 0.0 copy-done.2
  97.3 0.8 copy.27
Async XLA Ops:
  0.6 0.7 copy-start.3
  2.0 12.0 %copy-start = (bf16[64,1728]{1,0:T(8,128)(2,1)S(1)}, bf16[64,1728]{1,0:T(8,128)(2,1)}, u32[]{:S(2)}) copy-start(bf16[64,1728]{1,0:T(8,128)(2,1)} %k1_ref.1) | copy-start | bytes 663556
  16.2 1.1 %copy-start.1 = (bf16[64,1728]{1,0:T(8,128)(2,1)S(1)}, bf16[64,1728]{1,0:T(8,128)(2,1)}, u32[]{:S(2)}) copy-start(bf16[64,1728]{1,0:T(8,128)(2,1)} %k2_ref.1) | copy-start | bytes 663556
  95.4 1.9 %copy-start.2 = (f32[64,1728]{1,0:T(8,128)S(1)}, f32[64,1728]{1,0:T(8,128)}, u32[]{:S(2)}) copy-start(f32[64,1728]{1,0:T(8,128)} %get-tuple-element.39) | copy-start | bytes 1327108

commit v2 on v1

--- a/solution.py
+++ b/solution.py
@@ -16,6 +16,7 @@
 C = 64
 LANES = 128
 TAPS = 27
+VMEM_BYTES = 60 * 1024 * 1024
 MESH = pl.DeviceIdType.MESH
 BF = jnp.bfloat16
 F32 = jnp.float32
@@ -162,29 +163,47 @@
     return barrier
 
 
-def first_halo_kernel(space, x_ref, dy_ref, low_ref, up_ref, down_buf, back_buf, send_sem, recv_sem):
+def flip_kernels(k1_ref, k2_ref, f1_ref, f2_ref):
+    lo = lane_ids(C) < 64
+
+    def turned(tile):
+        lanes = slice(tile * LANES, min((tile + 1) * LANES, TAPS * C))
+        stacked = jnp.concatenate([k1_ref[:, lanes], k2_ref[:, lanes]], axis=0).astype(F32)
+        if stacked.shape[1] < LANES:
+            stacked = jnp.concatenate([stacked, stacked], axis=1)
+        return stacked.T
+
+    later = turned(13)
+    for tile in range(14):
+        here = later[0:C]
+        if tile < 13:
+            later = turned(12 - tile)
+            next_one = later[C : 2 * C]
+            lanes = slice(tile * LANES, (tile + 1) * LANES)
+            f1_ref[:, lanes] = jnp.where(lo, here, swap_halves(next_one)).astype(BF)
+            f2_ref[:, lanes] = jnp.where(lo, swap_halves(here), next_one).astype(BF)
+        else:
+            lanes = slice(tile * LANES, TAPS * C)
+            f1_ref[:, lanes] = here[:, 0:C].astype(BF)
+            f2_ref[:, lanes] = swap_halves(here)[:, 0:C].astype(BF)
+
+
+def first_halo_kernel(
+    space, x_ref, dy_ref, k1_ref, k2_ref, low_ref, up_ref, f1_ref, f2_ref,
+    down_buf, back_buf, send_sem, recv_sem,
+):
     barrier = greet(neighbours_ring(space))
     lo = lane_ids(C) < 64
     for n in range(HOME):
-        tx = to_tiles(pieces(x_ref[n]), lo)
-        ty = to_tiles(pieces(dy_ref[n]), lo)
-        down, back = halo_pack(tx, ty, lo)
-        down_buf[n] = down
-        back_buf[n] = back
+        first_x, first_dy = x_ref[n, :, 0:LANES], dy_ref[n, :, 0:LANES]
+        last_x, last_dy = x_ref[n, :, 3 * LANES :], dy_ref[n, :, 3 * LANES :]
+        down_buf[n] = jnp.where(lo, swap_halves(last_x), last_dy)
+        back_buf[n] = jnp.where(lo, first_dy, swap_halves(first_x))
     pl.semaphore_wait(barrier, 2)
     copies = exchange(down_buf, back_buf, low_ref, up_ref, send_sem, recv_sem, space)
     for copy in copies:
         copy.start()
-    for copy in copies:
-        copy.wait()
-
-
-def second_halo_kernel(space, down_ref, back_ref, low_ref, up_ref, send_sem, recv_sem):
-    barrier = greet(neighbours_ring(space))
-    pl.semaphore_wait(barrier, 2)
-    copies = exchange(down_ref, back_ref, low_ref, up_ref, send_sem, recv_sem, space)
-    for copy in copies:
-        copy.start()
+    flip_kernels(k1_ref, k2_ref, f1_ref, f2_ref)
     for copy in copies:
         copy.wait()
 
@@ -281,30 +300,85 @@
     wide = lane_ids(9 * C) < 64
     first_a, first_b = acc1[:, 0:LANES], acc1[:, LANES : 2 * LANES]
     second_a, second_b = acc2[:, 0:LANES], acc2[:, LANES : 2 * LANES]
-    sums_out[0 : 9 * C, :] = jnp.where(wide, first_b, second_b).astype(BF)
-    sums_out[9 * C : 18 * C, :] = jnp.where(wide, second_a, first_a).astype(BF)
-    sums_out[18 * C : 27 * C, :] = jnp.where(wide, first_a, second_a).astype(BF)
-    sums_out[27 * C : 2048, :] = jnp.zeros((2048 - 27 * C, LANES), BF)
+    parts = (
+        jnp.where(wide, first_b, second_b),
+        jnp.where(wide, second_a, first_a),
+        jnp.where(wide, first_a, second_a),
+    )
+    for tap in range(2 * 16):
+        if tap < TAPS:
+            at = tap % 9 * C
+            sums_out[tap // 16, tap % 16] = parts[tap // 9][at : at + C].astype(BF)
+        else:
+            sums_out[tap // 16, tap % 16] = zero
 
 
 def second_kernel(
-    x_ref, dy_ref, h_ref, g_ref, low_in, up_in, links_ref, count_ref, k2_ref, f1_ref,
-    sq_ref, sr_ref, sc_ref, out_ref, grad_ref,
+    space, x_ref, dy_ref, h_ref, g_ref, down_ref, back_ref, sums_ref, links_ref, count_ref,
+    k2_ref, f1_ref, sq_ref, sr_ref, sc_ref,
+    out_ref, grad_ref, arrived, total_ref,
     ht, gt, eh0, eh3, eg0, eg3, lh, lg, uh, ug, t_buf, dh, dg,
+    low_in, up_in, r0, s1, r1, p2, r2, q_buf, a2, chunk,
+    hs, hr, s0s, s0r, s1s, s1r, s2s, s2r, g2s, g2r, g1s, g1r, g0s, g0r, obs, obr,
 ):
-    lane = lane_ids(C)
-    lo = lane < 64
-    mats = (sq_ref, sr_ref, sc_ref)
-    unpack_halo(low_in, up_in, (lh, lg), (uh, ug))
+    batch = lax.axis_index("batch")
+    at = lax.axis_index("space")
+    y, z_lo = batch // 2, lax.rem(batch, 2)
+    x, inner = at // 8, lax.rem(at, 8)
+    z_hi, core = inner // 2, lax.rem(inner, 2)
+    other = 1 - core
+    g = x * 4 + y
+    z = z_hi * 2 + z_lo
+
+    def plane_peer(number):
+        return (lax.rem(number, 4) * 2 + z_lo, (number // 4) * 8 + inner)
+
+    def column_peer(number):
+        return (y * 2 + lax.rem(number, 2), x * 8 + (number // 2) * 2 + core)
+
+    def ring(step):
+        return (batch, lax.rem(at + space + step, space))
+
+    partner = (batch, x * 8 + z_hi * 2 + other)
+    plane = [plane_peer(lax.rem(g + d, 16)) for d in range(1, 16)]
+    column = [column_peer(lax.rem(z + d, 8)) for d in range(1, 8)]
+    barrier = greet([ring(1), ring(-1), ring(-1), ring(-2), ring(-3), partner] + column + plane)
+
+    def start(src, dst, sends, recvs, number, device):
+        copy = pltpu.make_async_remote_copy(
+            src_ref=src, dst_ref=dst, send_sem=sends.at[number], recv_sem=recvs.at[number],
+            device_id=device, device_id_type=MESH,
+        )
+        copy.start()
+        return copy
+
+    lo = lane_ids(C) < 64
     clear_last(ht, eh0, eh3)
     clear_last(gt, eg0, eg3)
-    count = count_ref[0, 0]
     for n in range(HOME):
         for src, tiles_ref, e0, e3 in ((h_ref, ht, eh0, eh3), (g_ref, gt, eg0, eg3)):
             for j in range(TILES):
                 tiles_ref[n, j] = src[n, j]
             e0[n] = swap_halves(src[n, 0])
             e3[n] = swap_halves(src[n, 3])
+    pl.semaphore_wait(barrier, 28)
+    halo = exchange(down_ref, back_ref, low_in, up_in, hs, hr, space)
+    for copy in halo:
+        copy.start()
+    pair = start(sums_ref.at[other], r0, s0s, s0r, 0, partner)
+    pair.wait_recv()
+    for d in range(16):
+        place = lax.rem(g + d, 16)
+        s1[place] = (sums_ref[core, place].astype(F32) + r0[place].astype(F32)).astype(BF)
+    scatter = [
+        start(s1.at[lax.rem(g + d, 16)], r1.at[d - 1], s1s, s1r, d - 1, plane[d - 1])
+        for d in range(1, 16)
+    ]
+    for copy in halo:
+        copy.wait_recv()
+    unpack_halo(low_in, up_in, (lh, lg), (uh, ug))
+    mats = (sq_ref, sr_ref, sc_ref)
+    count = count_ref[0, 0]
 
     def brick(n, _):
         build_columns(ht, eh0, eh3, lh, uh, links_ref, n, t_buf, dh, mats)
@@ -326,82 +400,62 @@
             grad_ref[n, :, lanes] = ((dy_ref[n, :, lanes].astype(F32) + term) * live).astype(BF)
         return 0
 
-    lax.fori_loop(0, HOME, brick, 0)
-
-
-def finish_kernel(
-    space, scale, s_ref, ob_ref, work_ref, one_ref, two_ref,
-    r1, p2, r2, q_buf, a2, chunk, a1, arrived, total,
-    s1s, s1r, s2s, s2r, g2s, g2r, g1s, g1r, obs, obr,
-):
-    batch = lax.axis_index("batch")
-    at = lax.axis_index("space")
-    y, z_lo = batch // 2, lax.rem(batch, 2)
-    x, inner = at // 8, lax.rem(at, 8)
-    g = x * 4 + y
-    h = z_lo * 8 + inner
-
-    def plane_peer(number):
-        return (lax.rem(number, 4) * 2 + z_lo, (number // 4) * 8 + inner)
-
-    def column_peer(number):
-        return (y * 2 + number // 8, x * 8 + lax.rem(number, 8))
-
-    def ring(step):
-        return (batch, lax.rem(at + space + step, space))
-
-    plane = [plane_peer(lax.rem(g + d, 16)) for d in range(1, 16)]
-    column = [column_peer(lax.rem(h + d, 16)) for d in range(1, 16)]
-    barrier = greet(plane + column + [ring(-1), ring(-2), ring(-3)])
-    pl.semaphore_wait(barrier, 33)
-
-    def start(src, dst, sends, recvs, number, device):
-        copy = pltpu.make_async_remote_copy(
-            src_ref=src, dst_ref=dst, send_sem=sends.at[number], recv_sem=recvs.at[number],
-            device_id=device, device_id_type=MESH,
-        )
-        copy.start()
-        return copy
-
-    scatter = [
-        start(s_ref.at[lax.rem(g + d, 16)], r1.at[d - 1], s1s, s1r, d - 1, plane[d - 1])
-        for d in range(1, 16)
-    ]
-    bricks = [
-        start(ob_ref.at[WORK_CAP + k], arrived.at[k], obs, obr, k, ring(k + 1)) for k in range(3)
-    ]
-    acc = s_ref[g].astype(F32)
+    lax.fori_loop(WORK_CAP, HOME, brick, 0)
+    acc = s1[g].astype(F32)
     for d in range(15):
         scatter[d].wait_recv()
         acc = acc + r1[d].astype(F32)
-    p2[...] = acc.reshape(16, 8, LANES)
+    p2[...] = acc.reshape(8, 8, LANES)
     column_scatter = [
-        start(p2.at[lax.rem(h + d, 16)], r2.at[d - 1], s2s, s2r, d - 1, column[d - 1])
-        for d in range(1, 16)
-    ]
-    piece = p2[h]
-    for d in range(15):
+        start(p2.at[lax.rem(z + d, 8)], r2.at[d - 1], s2s, s2r, d - 1, column[d - 1])
+        for d in range(1, 8)
+    ]
+    bricks = [
+        start(out_ref.at[WORK_CAP + k], arrived.at[k], obs, obr, k, ring(k + 1)) for k in range(3)
+    ]
+    lax.fori_loop(0, WORK_CAP, brick, 0)
+    piece = p2[z]
+    for d in range(7):
         column_scatter[d].wait_recv()
         piece = piece + r2[d]
     q_buf[...] = piece
-    a2[h] = piece
+    a2[z] = piece
     column_gather = [
-        start(q_buf, a2.at[h], g2s, g2r, d - 1, column[d - 1]) for d in range(1, 16)
-    ]
-    for d in range(15):
+        start(q_buf, a2.at[z], g2s, g2r, d - 1, column[d - 1]) for d in range(1, 8)
+    ]
+    for d in range(7):
         column_gather[d].wait_recv()
-    whole = a2[...].reshape(LANES, LANES).astype(BF)
+    whole = a2[...].reshape(C, LANES).astype(BF)
     chunk[...] = whole
-    a1[g] = whole
-    gather = [start(chunk, a1.at[g], g1s, g1r, d - 1, plane[d - 1]) for d in range(1, 16)]
-    for k in range(3):
-        bricks[k].wait_recv()
+    total_ref[core, g] = whole
+    gather = [
+        start(chunk, total_ref.at[core, g], g1s, g1r, d - 1, plane[d - 1]) for d in range(1, 16)
+    ]
+    forward = [start(chunk, total_ref.at[core, g], g0s, g0r, 0, partner)]
+    for d in range(1, 16):
+        gather[d - 1].wait_recv()
+        came = lax.rem(g + 16 - d, 16)
+        forward.append(
+            start(total_ref.at[core, came], total_ref.at[core, came], g0s, g0r, d, partner)
+        )
+    for copy in (*forward, *bricks):
+        copy.wait_recv()
+    for copy in (
+        *halo, pair, *scatter, *column_scatter, *column_gather, *gather, *forward, *bricks
+    ):
+        copy.wait_send()
+
+
+def finish_kernel(
+    scale, total_ref, ob_ref, arrived_ref, grad_ref, work_ref, grad_out, one_ref, two_ref, total
+):
+    grad_out[...] = grad_ref[...]
     work_ref[0] = ob_ref[0]
-    extra = arrived[0].astype(F32) + arrived[1].astype(F32) + arrived[2].astype(F32)
+    extra = (
+        arrived_ref[0].astype(F32) + arrived_ref[1].astype(F32) + arrived_ref[2].astype(F32)
+    )
     work_ref[1] = (ob_ref[1].astype(F32) + extra).astype(BF)
-    for d in range(15):
-        gather[d].wait_recv()
-    total[...] = a1[...].reshape(2048, LANES).astype(F32) * scale
+    total[...] = total_ref[...].reshape(2048, LANES).astype(F32) * scale
     lo = lane_ids(C) < 64
 
     def block(tap):
@@ -410,9 +464,9 @@
     def swapped(tap):
         return 9 <= tap < 18
 
-    def first_block(tap, low):
+    def first_block(tap):
         value = block(tap)
-        return value if swapped(tap) != low else swap_halves(value)
+        return swap_halves(value) if swapped(tap) else value
 
     def second_block(tap, low):
         value = block(TAPS - 1 - tap)
@@ -420,10 +474,10 @@
 
     for tile in range(14):
         tap = 2 * tile
-        here = first_block(tap, True)
+        here = first_block(tap)
         there = second_block(tap, True)
         if tap + 1 < TAPS:
-            pair = jnp.concatenate([here, first_block(tap + 1, True)], axis=0)
+            pair = jnp.concatenate([here, first_block(tap + 1)], axis=0)
             one_ref[:, tile * LANES : (tile + 1) * LANES] = pair.T[0:C, :]
             two_ref[:, tile * LANES : (tile + 1) * LANES] = jnp.where(
                 lo, there, second_block(tap + 1, False)
@@ -432,8 +486,6 @@
             pair = jnp.concatenate([here, here], axis=0)
             one_ref[:, tile * LANES : tile * LANES + C] = pair.T[0:C, 0:C]
             two_ref[:, tile * LANES : tile * LANES + C] = there[:, 0:C]
-    for copy in (*scatter, *column_scatter, *column_gather, *gather, *bricks):
-        copy.wait_send()
 
 
 def vmem():
@@ -446,12 +498,6 @@
 
 def bf_scratch(*shape):
     return pltpu.VMEM(shape, BF)
-
-
-def flip_kernel(kernel):
-    channels = kernel.shape[0]
-    taps = kernel.reshape(channels, TAPS, channels)[:, ::-1, :]
-    return taps.transpose(2, 1, 0).reshape(channels, TAPS * channels)
 
 
 def field_scratch():
@@ -461,75 +507,74 @@
     return tiles + rows + columns
 
 
-def halo_call(kernel, number, extra, args):
-    return pl.pallas_call(
-        kernel,
-        out_shape=[jax.ShapeDtypeStruct((HOME, C, LANES), BF)] * 2,
-        in_specs=[vmem()] * 2,
-        out_specs=[vmem()] * 2,
-        scratch_shapes=[*extra, pltpu.SemaphoreType.DMA((2,)), pltpu.SemaphoreType.DMA((2,))],
-        compiler_params=pltpu.CompilerParams(collective_id=number, has_side_effects=True),
-    )(*args)
-
-
 def shards(space, groups, features, cotangent, brick_count, destination, neighbours, kernel_one, kernel_two):
     x = features[0]
     dy = cotangent[0]
     mats = shift_matrices()
     halo = bf_scratch(HOME, C, LANES)
-    low, up = halo_call(functools.partial(first_halo_kernel, space), 0, [halo, halo], (x, dy))
     tile_shape = jax.ShapeDtypeStruct((HOME, TILES, C, LANES), BF)
     halo_shape = jax.ShapeDtypeStruct((HOME, C, LANES), BF)
-    local = pltpu.CompilerParams(vmem_limit_bytes=60 * 1024 * 1024)
+    bricks_shape = jax.ShapeDtypeStruct((HOME, C, TILES * LANES), BF)
+    flip_shape = jax.ShapeDtypeStruct((C, TAPS * C), BF)
+    sums_shape = jax.ShapeDtypeStruct((2, 16, C, LANES), BF)
+    dma = pltpu.SemaphoreType.DMA
+    low, up, flip_one, flip_two = pl.pallas_call(
+        functools.partial(first_halo_kernel, space),
+        out_shape=[halo_shape, halo_shape, flip_shape, flip_shape],
+        in_specs=[vmem()] * 4,
+        out_specs=[vmem()] * 4,
+        scratch_shapes=[halo, halo, dma((2,)), dma((2,))],
+        compiler_params=pltpu.CompilerParams(collective_id=0, has_side_effects=True),
+    )(x, dy, kernel_one, kernel_two)
     hidden, gpre, down, back, sums = pl.pallas_call(
         first_kernel,
-        out_shape=[
-            tile_shape, tile_shape, halo_shape, halo_shape,
-            jax.ShapeDtypeStruct((2048, LANES), BF),
-        ],
+        out_shape=[tile_shape, tile_shape, halo_shape, halo_shape, sums_shape],
         in_specs=[vmem()] * 4 + [smem()] * 2 + [vmem()] * 5,
         out_specs=[vmem()] * 5,
         scratch_shapes=field_scratch()
         + [bf_scratch(8, C, LANES)] * 2
         + [pltpu.VMEM((9 * C, 2 * LANES), F32)] * 2,
-        compiler_params=local,
-    )(x, dy, low, up, neighbours, brick_count, kernel_one, flip_kernel(kernel_two), *mats)
-    low, up = halo_call(functools.partial(second_halo_kernel, space), 1, [], (down, back))
-    bricks_shape = jax.ShapeDtypeStruct((HOME, C, TILES * LANES), BF)
-    out, grad_in = pl.pallas_call(
-        second_kernel,
-        out_shape=[bricks_shape, bricks_shape],
-        in_specs=[vmem()] * 6 + [smem()] * 2 + [vmem()] * 5,
-        out_specs=[vmem()] * 2,
-        scratch_shapes=field_scratch(),
-        compiler_params=local,
-    )(x, dy, hidden, gpre, low, up, neighbours, brick_count, kernel_two, flip_kernel(kernel_one), *mats)
+        compiler_params=pltpu.CompilerParams(vmem_limit_bytes=VMEM_BYTES),
+    )(x, dy, low, up, neighbours, brick_count, kernel_one, flip_two, *mats)
+    out, grad_in, arrived, total = pl.pallas_call(
+        functools.partial(second_kernel, space),
+        out_shape=[
+            bricks_shape, bricks_shape,
+            jax.ShapeDtypeStruct((3, C, TILES * LANES), BF), sums_shape,
+        ],
+        in_specs=[vmem()] * 7 + [smem()] * 2 + [vmem()] * 5,
+        out_specs=[vmem()] * 4,
+        scratch_shapes=field_scratch()
+        + [
+            halo, halo,
+            bf_scratch(16, C, LANES),
+            bf_scratch(16, C, LANES),
+            bf_scratch(15, C, LANES),
+            pltpu.VMEM((8, 8, LANES), F32),
+            pltpu.VMEM((7, 8, LANES), F32),
+            pltpu.VMEM((8, LANES), F32),
+            pltpu.VMEM((8, 8, LANES), F32),
+            bf_scratch(C, LANES),
+        ]
+        + [dma((n,)) for n in (2, 1, 15, 7, 7, 15, 16, 3) for _ in range(2)],
+        compiler_params=pltpu.CompilerParams(
+            collective_id=1, has_side_effects=True, vmem_limit_bytes=VMEM_BYTES
+        ),
+    )(x, dy, hidden, gpre, down, back, sums, neighbours, brick_count, kernel_two, flip_one, *mats)
     scale = 1.0 / math.sqrt(groups * space * HOME * TILES * LANES)
     grad_shape = jax.ShapeDtypeStruct((C, TAPS * C), F32)
-    dma = pltpu.SemaphoreType.DMA
-    work, grad_one, grad_two = pl.pallas_call(
-        functools.partial(finish_kernel, space, scale),
+    work, grad_out, grad_one, grad_two = pl.pallas_call(
+        functools.partial(finish_kernel, scale),
         out_shape=[
-            jax.ShapeDtypeStruct((WORK_CAP, C, TILES * LANES), BF), grad_shape, grad_shape,
+            jax.ShapeDtypeStruct((WORK_CAP, C, TILES * LANES), BF), bricks_shape,
+            grad_shape, grad_shape,
         ],
-        in_specs=[vmem()] * 2,
-        out_specs=[vmem()] * 3,
-        scratch_shapes=[
-            bf_scratch(15, LANES, LANES),
-            pltpu.VMEM((16, 8, LANES), F32),
-            pltpu.VMEM((15, 8, LANES), F32),
-            pltpu.VMEM((8, LANES), F32),
-            pltpu.VMEM((16, 8, LANES), F32),
-            bf_scratch(LANES, LANES),
-            bf_scratch(16, LANES, LANES),
-            bf_scratch(3, C, TILES * LANES),
-            pltpu.VMEM((2048, LANES), F32),
-        ]
-        + [dma((15,))] * 8
-        + [dma((3,))] * 2,
-        compiler_params=pltpu.CompilerParams(collective_id=2, has_side_effects=True),
-    )(sums.reshape(16, LANES, LANES), out)
-    return work[None], grad_in[None], grad_one, grad_two
+        in_specs=[vmem()] * 4,
+        out_specs=[vmem()] * 4,
+        scratch_shapes=[pltpu.VMEM((2048, LANES), F32)],
+        compiler_params=pltpu.CompilerParams(vmem_limit_bytes=VMEM_BYTES),
+    )(total, out, arrived, grad_in)
+    return work[None], grad_out[None], grad_one, grad_two
 
 
 def solution(mesh):

time: 99.7 us -> 70.6 us (0.71); the launches traced: 98 us -> 70.4 us
  Pallas kernels: 85.3 us -> 68.4 us
  local copies, waits for them, and re-layouts: 11.3 us -> 0.7 us
    pallas_call x4 -> x3, Pallas kernels: 71.7 us -> 54.8 us  [the longest x1 39.9 us: shards(): pl.pallas_call(functools.partial(second_kernel, space), out_shape=[bricks...]
    unnamed x12 -> x3, local copies, waits for them, and re-layouts: 4.93 us -> 0.7 us
    reshape x4 -> x0, local copies, waits for them, and re-layouts: 3.17 us -> none  [the longest x2 2.21 us: flip_kernel(): return taps.transpose(2, 1, 0).reshape(channels, TAPS * channels)]
    transpose x2 -> x0, local copies, waits for them, and re-layouts: 2.15 us -> none  [flip_kernel(): return taps.transpose(2, 1, 0).reshape(channels, TAPS * channels)]
    rev x2 -> x0, local copies, waits for them, and re-layouts: 1.06 us -> none  [flip_kernel(): taps = kernel.reshape(channels, TAPS, channels)[:, ::-1, :]]
where the time goes in v2:
time: 70.6 us; the launch traced here: 70.4 us
  Pallas kernels  68.4 us (97%)
  between operations  1.32 us (2%)
    pallas_call x1, Pallas kernels, shards(): pl.pallas_call(functools.partial(second_kernel, space), out_shape=[bricks...  39.9 us
    pallas_call x1, Pallas kernels, shards(): pl.pallas_call(first_kernel, out_shape=[tile_shape, tile_shape, halo_shap...  13.6 us
    pallas_call x1, Pallas kernels, shards(): pl.pallas_call(functools.partial(first_halo_kernel, space), out_shape=[ha...  12.2 us
    pallas_call x1, Pallas kernels, shards(): pl.pallas_call(functools.partial(finish_kernel, scale), out_shape=[jax.Sh...  2.68 us

profile of v2, /device:TPU:1, one launch (start us, length us, event | category | flops | bytes accessed | tf_op | source)
XLA Modules:
  0.0 70.4 jit_solution(12836231494120037353)
XLA Ops:
  0.6 0.0 copy-start
  1.3 0.0 copy-done
  1.3 0.7 copy.13.links_ref
  2.0 12.2 %shard_map.120 = (bf16[5,64,128]{2,1,0:T(8,128)(2,1)}, bf16[5,64,128]{2,1,0:T(8,128)(2,1)}, bf16[64,1728]{1,0:T(8,128)(2,1)}, bf16[64,1728]{1,0:T(8,128)(2,1)}) custom-call(bf16[5,64,512]{2,1,0:T(8,128)(2,1)} %bitcast.4, bf16[5,64,512]{2,1,0:T(8,128)(2,1)} %bitcast.7, bf16[64,1728]{1,0:T(8,128)(2,1)} %k1_ref.3, bf16[64,1728]{1,0:T(8,128)(2,1)} %k2_ref.3), custom_call_target="tpu_custom_call" | custom-call | tf_op jit(solution)/shard_map/pallas_call | solution.py:521
  14.3 13.6 %shard_map.121 = (bf16[5,4,64,128]{3,2,1,0:T(8,128)(2,1)}, bf16[5,4,64,128]{3,2,1,0:T(8,128)(2,1)}, bf16[5,64,128]{2,1,0:T(8,128)(2,1)}, bf16[5,64,128]{2,1,0:T(8,128)(2,1)}, bf16[2,16,64,128]{3,2,1,0:T(8,128)(2,1)}) custom-call(bf16[5,64,512]{2,1,0:T(8,128)(2,1)} %bitcast.5, bf16[5,64,512]{2,1,0:T(8,128)(2,1)} %bitcast.8, ...), custom_call_target="tpu_custom_call" | custom-call | tf_op jit(solution)/shard_map/pallas_call | solution.py:529
  27.9 39.9 %shard_map.122 = (bf16[5,64,512]{2,1,0:T(8,128)(2,1)}, bf16[5,64,512]{2,1,0:T(8,128)(2,1)}, bf16[3,64,512]{2,1,0:T(8,128)(2,1)}, bf16[2,16,64,128]{3,2,1,0:T(8,128)(2,1)}) custom-call(bf16[5,64,512]{2,1,0:T(8,128)(2,1)} %bitcast.6, bf16[5,64,512]{2,1,0:T(8,128)(2,1)} %bitcast.9, bf16[5,4,64,128]{3,2,1,0:T(8,128)(2,1)} %get-tuple-element.24.h_ref, ...), custom_call_target="tpu_custom_call" | custom-call | tf_op jit(solution)/shard_map/pallas_call | solution.py:539
  67.7 2.7 %shard_map.123 = (bf16[2,64,512]{2,1,0:T(8,128)(2,1)}, bf16[5,64,512]{2,1,0:T(8,128)(2,1)}, f32[64,1728]{1,0:T(8,128)}, f32[64,1728]{1,0:T(8,128)}) custom-call(bf16[2,16,64,128]{3,2,1,0:T(8,128)(2,1)} %get-tuple-element.30.total_ref, bf16[5,64,512]{2,1,0:T(8,128)(2,1)} %get-tuple-element.31.ob_ref, bf16[3,64,512]{2,1,0:T(8,128)(2,1)} %get-tuple-element.32.arrived_ref, ...), custom_call_target="tpu_custom_call" | custom-call | tf_op jit(solution)/shard_map/pallas_call | solution.py:566
Async XLA Ops:
  0.6 0.7 copy-start

commit v3 on v2

v3 whole, which is shorter than its diff:
```python
import functools
import math

import jax
import jax.numpy as jnp
import numpy as np
from jax import lax
from jax.experimental import pallas as pl
from jax.experimental.pallas import tpu as pltpu
from jax.sharding import PartitionSpec as P

WORK_CAP = 2
HOME = 5
TILES = 4
SPAN = 6
C = 64
LANES = 128
TAPS = 27
VMEM_BYTES = 60 * 1024 * 1024
MESH = pl.DeviceIdType.MESH
BF = jnp.bfloat16
F32 = jnp.float32


def shift_matrices():
    def column(q, r, blocks):
        m = np.zeros((len(blocks) * LANES, LANES), np.float32)
        for half in range(2):
            for b in range(8):
                for c in range(8):
                    bb, cc = b + q, c + r
                    kind = (2 if not 0 <= cc < 8 else 0) + (1 if not 0 <= bb < 8 else 0)
                    at = blocks.index(kind) * LANES + half * 64 + (bb % 8) * 8 + cc % 8
                    m[at, half * 64 + b * 8 + c] = 1.0
        return m

    s_q = np.concatenate([column(-1, 0, [1, 0]), column(1, 0, [1, 0])], axis=1)
    s_r = np.concatenate([column(0, -1, [0, 2]), column(0, 1, [0, 2])], axis=1)
    s_c = np.concatenate(
        [column(q, r, [1, 0, 2, 3]) for q, r in ((-1, -1), (-1, 1), (1, -1), (1, 1))], axis=1
    )
    return [jnp.asarray(m, BF) for m in (s_q, s_r, s_c)]


def lane_ids(rows):
    return lax.broadcasted_iota(jnp.int32, (rows, LANES), 1)


def swap_halves(v):
    return pltpu.roll(v, 64, 1)


def to_tiles(parts, lo):
    n0, n1, n2, n3 = parts
    return [
        jnp.where(lo, n0, swap_halves(n2)),
        jnp.where(lo, swap_halves(n0), n2),
        jnp.where(lo, n1, swap_halves(n3)),
        jnp.where(lo, swap_halves(n1), n3),
    ]


def from_tiles(tiles, lo):
    f0, f1, f2, f3 = tiles
    return [
        jnp.where(lo, f0, swap_halves(f1)),
        jnp.where(lo, f2, swap_halves(f3)),
        jnp.where(lo, swap_halves(f0), f1),
        jnp.where(lo, swap_halves(f2), f3),
    ]


def pieces(value):
    return [value[:, k * LANES : (k + 1) * LANES] for k in range(TILES)]


def offset_number(p, q, r):
    number = 9 * (p + 1) + 3 * (q + 1) + (r + 1)
    return number if number < 13 else number - 1


def build_columns(fields, planes, links_ref, n, t_ref, mats):
    s_q, s_r, s_c = mats
    lane = lane_ids(C)
    lo = lane < 64
    row = (lane % 64) // 8
    col = lane % 8

    def slot(p, q, r):
        if (p, q, r) == (0, 0, 0):
            return n
        found = links_ref[0, offset_number(p, q, r), n]
        return jnp.where(found < 0, HOME, found)

    slots = {
        (p, q, r): slot(p, q, r) for p in (-1, 0, 1) for q in (-1, 0, 1) for r in (-1, 0, 1)
    }
    zero = jnp.zeros((C, LANES), BF)
    where = []
    for tiles_ref, e0_ref, e3_ref, low_ref, up_ref, d_ref in fields:

        def source(k, q, r):
            if k == 0:
                return jnp.where(lo, low_ref[slots[-1, q, r]], e3_ref[slots[0, q, r]])
            if k == SPAN - 1:
                return jnp.where(lo, e0_ref[slots[0, q, r]], up_ref[slots[1, q, r]])
            return tiles_ref[slots[0, q, r], k - 1]

        for k in planes:
            t1 = source(k, 0, 0)
            t2 = jnp.where(row == 0, source(k, 1, 0), jnp.where(row == 7, source(k, -1, 0), zero))
            t3 = jnp.where(col == 7, source(k, 0, -1), jnp.where(col == 0, source(k, 0, 1), zero))
            above = jnp.where(col == 7, source(k, -1, -1), jnp.where(col == 0, source(k, -1, 1), zero))
            below = jnp.where(col == 7, source(k, 1, -1), jnp.where(col == 0, source(k, 1, 1), zero))
            t4 = jnp.where(row == 7, above, jnp.where(row == 0, below, zero))
            rows = slice(len(where) * C, (len(where) + 1) * C)
            t_ref[rows, 0:LANES] = t2
            t_ref[rows, LANES : 2 * LANES] = t1
            t_ref[rows, 2 * LANES : 3 * LANES] = t3
            t_ref[rows, 3 * LANES : 4 * LANES] = t4
            d_ref[n, k, 4 * C : 5 * C, :] = t1
            where.append((d_ref, k))
    used = slice(0, len(where) * C)

    def put(result, order):
        packed = result.astype(BF)
        for place, qr in enumerate(order):
            for i, (d_ref, k) in enumerate(where):
                d_ref[n, k, qr * C : (qr + 1) * C, :] = packed[
                    i * C : (i + 1) * C, place * LANES : (place + 1) * LANES
                ]

    put(jnp.dot(t_ref[used, 0 : 2 * LANES], s_q[...], preferred_element_type=F32), (1, 7))
    put(jnp.dot(t_ref[used, LANES : 3 * LANES], s_r[...], preferred_element_type=F32), (3, 5))
    put(jnp.dot(t_ref[used, :], s_c[...], preferred_element_type=F32), (0, 2, 6, 8))


def halo_pack(tiles_a, tiles_b, lo):
    down = jnp.where(lo, swap_halves(tiles_a[3]), tiles_b[3])
    back = jnp.where(lo, tiles_b[0], swap_halves(tiles_a[0]))
    return down, back


def neighbours_ring(space):
    me = lax.axis_index("space")
    batch = lax.axis_index("batch")
    return (batch, lax.rem(me + 1, space)), (batch, lax.rem(me + space - 1, space))


def exchange(down_ref, back_ref, low_ref, up_ref, send_sem, recv_sem, space):
    following, previous = neighbours_ring(space)
    forward = pltpu.make_async_remote_copy(
        src_ref=down_ref, dst_ref=low_ref, send_sem=send_sem.at[0], recv_sem=recv_sem.at[0],
        device_id=following, device_id_type=MESH,
    )
    backward = pltpu.make_async_remote_copy(
        src_ref=back_ref, dst_ref=up_ref, send_sem=send_sem.at[1], recv_sem=recv_sem.at[1],
        device_id=previous, device_id_type=MESH,
    )
    return forward, backward


def greet(devices):
    barrier = pltpu.get_barrier_semaphore()
    for device in devices:
        pl.semaphore_signal(barrier, inc=1, device_id=device, device_id_type=MESH)
    return barrier


def flip_kernels(k1_ref, k2_ref, f1_ref, f2_ref):
    lo = lane_ids(C) < 64

    def turned(tile):
        lanes = slice(tile * LANES, min((tile + 1) * LANES, TAPS * C))
        stacked = jnp.concatenate([k1_ref[:, lanes], k2_ref[:, lanes]], axis=0).astype(F32)
        if stacked.shape[1] < LANES:
            stacked = jnp.concatenate([stacked, stacked], axis=1)
        return stacked.T

    later = turned(13)
    for tile in range(14):
        here = later[0:C]
        if tile < 13:
            later = turned(12 - tile)
            next_one = later[C : 2 * C]
            lanes = slice(tile * LANES, (tile + 1) * LANES)
            f1_ref[:, lanes] = jnp.where(lo, here, swap_halves(next_one)).astype(BF)
            f2_ref[:, lanes] = jnp.where(lo, swap_halves(here), next_one).astype(BF)
        else:
            lanes = slice(tile * LANES, TAPS * C)
            f1_ref[:, lanes] = here[:, 0:C].astype(BF)
            f2_ref[:, lanes] = swap_halves(here)[:, 0:C].astype(BF)


def unpack_halo(low_in, up_in, lows, ups):
    for n in range(HOME):
        lows[0][n] = low_in[n]
        lows[1][n] = swap_halves(low_in[n])
        ups[0][n] = up_in[n]
        ups[1][n] = swap_halves(up_in[n])
    zero = jnp.zeros((C, LANES), BF)
    for ref in (*lows, *ups):
        ref[HOME] = zero


def clear_last(tiles_ref, e0_ref, e3_ref):
    zero = jnp.zeros((C, LANES), BF)
    for j in range(TILES):
        tiles_ref[HOME, j] = zero
    e0_ref[HOME] = zero
    e3_ref[HOME] = zero


INNER = (1, 2, 3, 4)
EDGE = (0, 5)


def hops(step, size):
    return min(step, size - step)


def block_kernel(
    space, x_ref, dy_ref, links_ref, count_ref, k1_hbm, k2_hbm, sq_hbm, sr_hbm, sc_hbm,
    out_ref, grad_ref, arrived, total_ref,
    xt, yt, ex0, ex3, ey0, ey3, lx, ly, ux, uy,
    ht, gt, eh0, eh3, eg0, eg3, lh, lg, uh, ug,
    t_buf, dx, dd, gpad, hpad, acc1, acc2,
    k1_ref, k2_ref, sq_ref, sr_ref, sc_ref, f1_ref, f2_ref,
    down1, back1, down2, back2, low1, up1, low2, up2, sums32, sums16,
    r0, s1, r1, p2, r2, q_buf, a2, chunk,
    local, h1s, h1r, h2s, h2r, s0s, s0r, s1s, s1r, s2s, s2r, g2s, g2r, g1s, g1r, g0s, g0r, obs, obr,
):
    batch = lax.axis_index("batch")
    at = lax.axis_index("space")
    y, z_lo = batch // 2, lax.rem(batch, 2)
    x, inner = at // 8, lax.rem(at, 8)
    z_hi, core = inner // 2, lax.rem(inner, 2)
    other = 1 - core
    g = x * 4 + y
    z = z_hi * 2 + z_lo

    def ring(step):
        return (batch, lax.rem(at + space + step, space))

    def plane_at(step, sign=1):
        px = lax.rem(x + 4 + sign * (step // 4), 4)
        py = lax.rem(y + 4 + sign * (step % 4), 4)
        return px, py

    def plane_place(step, sign=1):
        px, py = plane_at(step, sign)
        return px * 4 + py

    def plane_peer(step):
        px, py = plane_at(step)
        return (py * 2 + z_lo, px * 8 + inner)

    def column_place(step):
        return lax.rem(z + step, 8)

    def column_peer(step):
        pz = column_place(step)
        return (y * 2 + lax.rem(pz, 2), x * 8 + (pz // 2) * 2 + core)

    near_plane = sorted(range(1, 16), key=lambda i: (hops(i // 4, 4) + hops(i % 4, 4), i))
    near_column = sorted(range(1, 8), key=lambda i: (hops(i, 8), i))
    far_plane, far_column = near_plane[::-1], near_column[::-1]
    partner = (batch, x * 8 + z_hi * 2 + other)
    barrier = greet(
        [ring(1), ring(-1), ring(-1), ring(-2), ring(-3), partner]
        + [column_peer(i) for i in far_column]
        + [plane_peer(i) for i in far_plane]
    )
    loads = [
        pltpu.make_async_copy(src, dst, local.at[i])
        for i, (src, dst) in enumerate(
            ((k1_hbm, k1_ref), (k2_hbm, k2_ref), (sq_hbm, sq_ref), (sr_hbm, sr_ref), (sc_hbm, sc_ref))
        )
    ]
    for load in loads:
        load.start()

    def start(src, dst, sends, recvs, number, device):
        copy = pltpu.make_async_remote_copy(
            src_ref=src, dst_ref=dst, send_sem=sends.at[number], recv_sem=recvs.at[number],
            device_id=device, device_id_type=MESH,
        )
        copy.start()
        return copy

    lo = lane_ids(C) < 64
    zero = jnp.zeros((C, LANES), BF)
    mats = (sq_ref, sr_ref, sc_ref)
    count = count_ref[0, 0]
    for n in range(HOME):
        first_x, first_dy = x_ref[n, :, 0:LANES], dy_ref[n, :, 0:LANES]
        last_x, last_dy = x_ref[n, :, 3 * LANES :], dy_ref[n, :, 3 * LANES :]
        down1[n] = jnp.where(lo, swap_halves(last_x), last_dy)
        back1[n] = jnp.where(lo, first_dy, swap_halves(first_x))
    pl.semaphore_wait(barrier, 28)
    halo1 = exchange(down1, back1, low1, up1, h1s, h1r, space)
    for copy in halo1:
        copy.start()

    for tiles_ref, e0, e3 in ((xt, ex0, ex3), (yt, ey0, ey3), (ht, eh0, eh3), (gt, eg0, eg3)):
        clear_last(tiles_ref, e0, e3)
    for n in range(HOME):
        live = jnp.where(n < count, 1.0, 0.0).astype(F32)
        for src, tiles_ref, e0, e3 in ((x_ref, xt, ex0, ex3), (dy_ref, yt, ey0, ey3)):
            masked = (src[n].astype(F32) * live).astype(BF)
            tiles = to_tiles(pieces(masked), lo)
            for j in range(TILES):
                tiles_ref[n, j] = tiles[j]
            e0[n] = swap_halves(tiles[0])
            e3[n] = swap_halves(tiles[3])
    for ref in (gpad, hpad):
        for j in (0, 1, 6, 7):
            ref[j] = zero
    acc1[...] = jnp.zeros_like(acc1)
    acc2[...] = jnp.zeros_like(acc2)
    for load in loads:
        load.wait()
    field_x = (xt, ex0, ex3, lx, ux, dx)
    field_y = (yt, ey0, ey3, ly, uy, dd)
    field_h = (ht, eh0, eh3, lh, uh, dx)
    field_g = (gt, eg0, eg3, lg, ug, dd)

    def first_inner(n, _):
        build_columns((field_x, field_y), INNER, links_ref, n, t_buf, mats)
        return 0

    lax.fori_loop(0, HOME, first_inner, 0)
    flip_kernels(k1_ref, k2_ref, f1_ref, f2_ref)
    for copy in halo1:
        copy.wait_recv()
    unpack_halo(low1, up1, (lx, ly), (ux, uy))

    def first_brick(n, _):
        build_columns((field_x, field_y), EDGE, links_ref, n, t_buf, mats)
        hidden = []
        grads = []
        for j in range(TILES):
            pre = jnp.dot(
                k1_ref[...], dx[n, j : j + 3].reshape(TAPS * C, LANES), preferred_element_type=F32
            )
            grad_hidden = jnp.dot(
                f2_ref[...], dd[n, j : j + 3].reshape(TAPS * C, LANES), preferred_element_type=F32
            )
            sigma = 1.0 / (1.0 + jnp.exp(-pre))
            hid = (pre * sigma).astype(BF)
            gpre = (grad_hidden * (sigma * (1.0 + pre * (1.0 - sigma)))).astype(BF)
            ht[n, j] = hid
            gt[n, j] = gpre
            hpad[j + 2] = hid
            gpad[j + 2] = gpre
            hidden.append(hid)
            grads.append(gpre)
        for tiles, e0, e3 in ((hidden, eh0, eh3), (grads, eg0, eg3)):
            e0[n] = swap_halves(tiles[0])
            e3[n] = swap_halves(tiles[3])
        down, back = halo_pack(hidden, grads, lo)
        down2[n] = down
        back2[n] = back
        for acc, cols, pad, flip in ((acc1, dx, gpad, False), (acc2, dd, hpad, True)):
            total = acc[...]
            for k in (0, 2, 4):
                left = jnp.concatenate([cols[n, k], cols[n, k + 1]], axis=1)

                def right(at):
                    if flip:
                        return jnp.concatenate([pad[at + 1], pad[at], zero, pad[at + 2]], axis=0)
                    return jnp.concatenate([pad[at], pad[at + 1], pad[at + 2], zero], axis=0)

                both = jnp.concatenate([right(k), right(k + 1)], axis=1)
                total = total + lax.dot_general(
                    left, both, (((1,), (1,)), ((), ())), preferred_element_type=F32
                )
            acc[...] = total
        return 0

    lax.fori_loop(0, HOME, first_brick, 0)
    wide = lane_ids(9 * C) < 64
    first_a, first_b = acc1[:, 0:LANES], acc1[:, LANES : 2 * LANES]
    second_a, second_b = acc2[:, 0:LANES], acc2[:, LANES : 2 * LANES]
    parts = (
        jnp.where(wide, first_b, second_b),
        jnp.where(wide, second_a, first_a),
        jnp.where(wide, first_a, second_a),
    )
    for tap in range(2 * 16):
        if tap < TAPS:
            row = tap % 9 * C
            value = parts[tap // 9][row : row + C]
        else:
            value = jnp.zeros((C, LANES), F32)
        sums32[tap // 16, tap % 16] = value
        sums16[tap // 16, tap % 16] = value.astype(BF)
    pair = start(sums16.at[other], r0, s0s, s0r, 0, partner)
    halo2 = exchange(down2, back2, low2, up2, h2s, h2r, space)
    for copy in halo2:
        copy.start()

    def second_inner(n, _):
        build_columns((field_h, field_g), INNER, links_ref, n, t_buf, mats)
        return 0

    lax.fori_loop(0, WORK_CAP, second_inner, 0)
    pair.wait_recv()
    for d in far_plane + [0]:
        place = plane_place(d)
        s1[place] = (sums32[core, place] + r0[place].astype(F32)).astype(BF)
    scatter = {
        d: start(s1.at[plane_place(d)], r1.at[d - 1], s1s, s1r, d - 1, plane_peer(d))
        for d in far_plane
    }
    lax.fori_loop(WORK_CAP, HOME, second_inner, 0)
    for copy in halo2:
        copy.wait_recv()
    unpack_halo(low2, up2, (lh, lg), (uh, ug))

    def second_brick(n, _):
        build_columns((field_h, field_g), EDGE, links_ref, n, t_buf, mats)
        mixed = []
        backs = []
        for j in range(TILES):
            mixed.append(jnp.dot(
                k2_ref[...], dx[n, j : j + 3].reshape(TAPS * C, LANES), preferred_element_type=F32
            ))
            backs.append(jnp.dot(
                f1_ref[...], dd[n, j : j + 3].reshape(TAPS * C, LANES), preferred_element_type=F32
            ))
        live = jnp.where(n < count, 1.0, 0.0).astype(F32)
        for k, (m, b) in enumerate(zip(from_tiles(mixed, lo), from_tiles(backs, lo))):
            lanes = slice(k * LANES, (k + 1) * LANES)
            out_ref[n, :, lanes] = ((x_ref[n, :, lanes].astype(F32) + m) * live).astype(BF)
            term = b.astype(BF).astype(F32)
            grad_ref[n, :, lanes] = ((dy_ref[n, :, lanes].astype(F32) + term) * live).astype(BF)
        return 0

    lax.fori_loop(WORK_CAP, HOME, second_brick, 0)
    acc = s1[g].astype(F32)
    for d in near_plane:
        scatter[d].wait_recv()
        acc = acc + r1[d - 1].astype(F32)
    p2[...] = acc.reshape(8, 8, LANES)
    column_scatter = {
        d: start(p2.at[column_place(d)], r2.at[d - 1], s2s, s2r, d - 1, column_peer(d))
        for d in far_column
    }
    bricks = [
        start(out_ref.at[WORK_CAP + k], arrived.at[k], obs, obr, k, ring(k + 1)) for k in range(3)
    ]
    lax.fori_loop(0, WORK_CAP, second_brick, 0)
    piece = p2[z]
    for d in near_column:
        column_scatter[d].wait_recv()
        piece = piece + r2[d - 1]
    q_buf[...] = piece
    a2[z] = piece
    column_gather = {
        d: start(q_buf, a2.at[z], g2s, g2r, d - 1, column_peer(d)) for d in far_column
    }
    for d in near_column:
        column_gather[d].wait_recv()
    whole = a2[...].reshape(C, LANES).astype(BF)
    chunk[...] = whole
    total_ref[core, g] = whole
    gather = {
        d: start(chunk, total_ref.at[core, g], g1s, g1r, d - 1, plane_peer(d)) for d in far_plane
    }
    forward = [start(chunk, total_ref.at[core, g], g0s, g0r, 0, partner)]
    for d in near_plane:
        gather[d].wait_recv()
        came = plane_place(d, -1)
        forward.append(
            start(total_ref.at[core, came], total_ref.at[core, came], g0s, g0r, d, partner)
        )
    for copy in (*forward, *bricks):
        copy.wait_recv()
    for copy in (
        *halo1, *halo2, pair, *scatter.values(), *column_scatter.values(),
        *column_gather.values(), *gather.values(), *forward, *bricks,
    ):
        copy.wait_send()


def finish_kernel(
    scale, total_ref, ob_ref, arrived_ref, grad_ref, work_ref, grad_out, one_ref, two_ref, total
):
    grad_out[...] = grad_ref[...]
    work_ref[0] = ob_ref[0]
    extra = (
        arrived_ref[0].astype(F32) + arrived_ref[1].astype(F32) + arrived_ref[2].astype(F32)
    )
    work_ref[1] = (ob_ref[1].astype(F32) + extra).astype(BF)
    total[...] = total_ref[...].reshape(2048, LANES).astype(F32) * scale
    lo = lane_ids(C) < 64

    def block(tap):
        return total[tap * C : (tap + 1) * C, :]

    def swapped(tap):
        return 9 <= tap < 18

    def first_block(tap):
        value = block(tap)
        return swap_halves(value) if swapped(tap) else value

    def second_block(tap, low):
        value = block(TAPS - 1 - tap)
        return value if swapped(tap) == low else swap_halves(value)

    for tile in range(14):
        tap = 2 * tile
        here = first_block(tap)
        there = second_block(tap, True)
        if tap + 1 < TAPS:
            pair = jnp.concatenate([here, first_block(tap + 1)], axis=0)
            one_ref[:, tile * LANES : (tile + 1) * LANES] = pair.T[0:C, :]
            two_ref[:, tile * LANES : (tile + 1) * LANES] = jnp.where(
                lo, there, second_block(tap + 1, False)
            )
        else:
            pair = jnp.concatenate([here, here], axis=0)
            one_ref[:, tile * LANES : tile * LANES + C] = pair.T[0:C, 0:C]
            two_ref[:, tile * LANES : tile * LANES + C] = there[:, 0:C]


def vmem():
    return pl.BlockSpec(memory_space=pltpu.VMEM)


def smem():
    return pl.BlockSpec(memory_space=pltpu.SMEM)


def bf_scratch(*shape):
    return pltpu.VMEM(shape, BF)


def shards(space, groups, features, cotangent, brick_count, destination, neighbours, kernel_one, kernel_two):
    bricks_shape = jax.ShapeDtypeStruct((HOME, C, TILES * LANES), BF)
    sums_shape = jax.ShapeDtypeStruct((2, 16, C, LANES), BF)
    dma = pltpu.SemaphoreType.DMA
    tiles = bf_scratch(HOME + 1, TILES, C, LANES)
    rows = bf_scratch(HOME + 1, C, LANES)
    field = [tiles] * 2 + [rows] * 8
    anywhere = pl.BlockSpec(memory_space=pl.ANY)
    kernel_rows = bf_scratch(C, TAPS * C)
    out, grad_in, arrived, total = pl.pallas_call(
        functools.partial(block_kernel, space),
        out_shape=[
            bricks_shape, bricks_shape,
            jax.ShapeDtypeStruct((3, C, TILES * LANES), BF), sums_shape,
        ],
        in_specs=[vmem()] * 2 + [smem()] * 2 + [anywhere] * 5,
        out_specs=[vmem()] * 4,
        scratch_shapes=field
        + field
        + [bf_scratch(2 * TILES * C, 4 * LANES)]
        + [bf_scratch(HOME, SPAN, 9 * C, LANES)] * 2
        + [bf_scratch(8, C, LANES)] * 2
        + [pltpu.VMEM((9 * C, 2 * LANES), F32)] * 2
        + [kernel_rows] * 2
        + [bf_scratch(2 * LANES, 2 * LANES)] * 2
        + [bf_scratch(4 * LANES, 4 * LANES)]
        + [kernel_rows] * 2
        + [bf_scratch(HOME, C, LANES)] * 8
        + [pltpu.VMEM((2, 16, C, LANES), F32), bf_scratch(2, 16, C, LANES)]
        + [
            bf_scratch(16, C, LANES),
            bf_scratch(16, C, LANES),
            bf_scratch(15, C, LANES),
            pltpu.VMEM((8, 8, LANES), F32),
            pltpu.VMEM((7, 8, LANES), F32),
            pltpu.VMEM((8, LANES), F32),
            pltpu.VMEM((8, 8, LANES), F32),
            bf_scratch(C, LANES),
        ]
        + [dma((5,))]
        + [dma((n,)) for n in (2, 2, 1, 15, 7, 7, 15, 16, 3) for _ in range(2)],
        compiler_params=pltpu.CompilerParams(
            collective_id=0, has_side_effects=True, vmem_limit_bytes=VMEM_BYTES
        ),
    )(features[0], cotangent[0], neighbours, brick_count, kernel_one, kernel_two, *shift_matrices())
    scale = 1.0 / math.sqrt(groups * space * HOME * TILES * LANES)
    grad_shape = jax.ShapeDtypeStruct((C, TAPS * C), F32)
    work, grad_out, grad_one, grad_two = pl.pallas_call(
        functools.partial(finish_kernel, scale),
        out_shape=[
            jax.ShapeDtypeStruct((WORK_CAP, C, TILES * LANES), BF), bricks_shape,
            grad_shape, grad_shape,
        ],
        in_specs=[vmem()] * 4,
        out_specs=[vmem()] * 4,
        scratch_shapes=[pltpu.VMEM((2048, LANES), F32)],
        compiler_params=pltpu.CompilerParams(vmem_limit_bytes=VMEM_BYTES),
    )(total, out, arrived, grad_in)
    return work[None], grad_out[None], grad_one, grad_two


def solution(mesh):
    return jax.shard_map(
        functools.partial(shards, mesh.shape["space"], mesh.shape["batch"]),
        mesh=mesh,
        in_specs=(
            P("batch", "space", None, None),
            P("batch", "space", None, None),
            P("batch", "space"),
            P("batch", "space"),
            P("batch", None, "space"),
            P(),
            P(),
        ),
        out_specs=(P("batch", "space", None, None), P("batch", "space", None, None), P(), P()),
        check_vma=False,
    )
```

time: 70.6 us -> 59.2 us (0.84)
  Pallas kernels: 68.4 us -> 57 us
    pallas_call x3 -> x1, Pallas kernels: 65.7 us -> 54.3 us  [shards(): pl.pallas_call(functools.partial(block_kernel, space), out_shape=[bricks_...]
where the time goes in v3:
time: 59.2 us; the launch traced here: 59 us
  Pallas kernels  57 us (96%)
  between operations  1.31 us (2%)
  local copies, waits for them, and re-layouts  0.71 us (1%)
    pallas_call x1, Pallas kernels, shards(): pl.pallas_call(functools.partial(block_kernel, space), out_shape=[bricks_...  54.3 us
    pallas_call x1, Pallas kernels, shards(): pl.pallas_call(functools.partial(finish_kernel, scale), out_shape=[jax.Sh...  2.68 us

profile of v3, /device:TPU:1, one launch (start us, length us, event | category | flops | bytes accessed | tf_op | source)
XLA Modules:
  0.0 59.0 jit_solution(13489501140600788189)
XLA Ops:
  0.6 0.0 copy-start
  1.3 0.0 copy-done
  1.3 0.7 %copy.13.links_ref = s32[1,26,5]{2,1,0:T(8,128)} copy(s32[1,26,5]{1,0,2:T(1,128)S(1)} %copy-done) | data formatting | bytes 1040 | tf_op args[4]
  2.0 54.3 %shard_map.120 = (bf16[5,64,512]{2,1,0:T(8,128)(2,1)}, bf16[5,64,512]{2,1,0:T(8,128)(2,1)}, bf16[3,64,512]{2,1,0:T(8,128)(2,1)}, bf16[2,16,64,128]{3,2,1,0:T(8,128)(2,1)}) custom-call(bf16[5,64,512]{2,1,0:T(8,128)(2,1)} %bitcast.4, bf16[5,64,512]{2,1,0:T(8,128)(2,1)} %bitcast.5, s32[1,26,5]{2,1,0:T(8,128)} %copy.13.links_ref, s32[1,1]{1,0:T(1,128)S(6)} %copy.14.count_ref, ...), custom_call_target="tpu_custom_call" | custom-call | tf_op jit(solution)/shard_map/pallas_call | solution.py:550
  56.4 2.7 %shard_map.121 = (bf16[2,64,512]{2,1,0:T(8,128)(2,1)}, bf16[5,64,512]{2,1,0:T(8,128)(2,1)}, f32[64,1728]{1,0:T(8,128)}, f32[64,1728]{1,0:T(8,128)}) custom-call(bf16[2,16,64,128]{3,2,1,0:T(8,128)(2,1)} %get-tuple-element.12.total_ref, bf16[5,64,512]{2,1,0:T(8,128)(2,1)} %get-tuple-element.13.ob_ref, bf16[3,64,512]{2,1,0:T(8,128)(2,1)} %get-tuple-element.14.arrived_ref, ...), custom_call_target="tpu_custom_call" | custom-call | tf_op jit(solution)/shard_map/pallas_call | solution.py:588
Async XLA Ops:
  0.6 0.7 %copy-start = (s32[1,26,5]{1,0,2:T(1,128)S(1)}, s32[1,26,5]{1,0,2:T(1,128)}, u32[]{:S(2)}) copy-start(s32[1,26,5]{1,0,2:T(1,128)} %param.13) | copy-start | bytes 1564

commit v4 on v3

--- a/solution.py
+++ b/solution.py
@@ -16,7 +16,7 @@
 C = 64
 LANES = 128
 TAPS = 27
-VMEM_BYTES = 60 * 1024 * 1024
+VMEM_BYTES = 32 * 1024 * 1024
 MESH = pl.DeviceIdType.MESH
 BF = jnp.bfloat16
 F32 = jnp.float32
@@ -89,7 +89,7 @@
     def slot(p, q, r):
         if (p, q, r) == (0, 0, 0):
             return n
-        found = links_ref[0, offset_number(p, q, r), n]
+        found = links_ref[n, 0, offset_number(p, q, r)]
         return jnp.where(found < 0, HOME, found)
 
     slots = {
@@ -220,15 +220,15 @@
 
 
 def block_kernel(
-    space, x_ref, dy_ref, links_ref, count_ref, k1_hbm, k2_hbm, sq_hbm, sr_hbm, sc_hbm,
+    space, x_hbm, dy_hbm, links_hbm, count_ref, k1_hbm, k2_hbm, sq_hbm, sr_hbm, sc_hbm,
     out_ref, grad_ref, arrived, total_ref,
     xt, yt, ex0, ex3, ey0, ey3, lx, ly, ux, uy,
     ht, gt, eh0, eh3, eg0, eg3, lh, lg, uh, ug,
-    t_buf, dx, dd, gpad, hpad, acc1, acc2,
+    t_buf, dx, dd, acc1, acc2,
     k1_ref, k2_ref, sq_ref, sr_ref, sc_ref, f1_ref, f2_ref,
     down1, back1, down2, back2, low1, up1, low2, up2, sums32, sums16,
     r0, s1, r1, p2, r2, q_buf, a2, chunk,
-    local, h1s, h1r, h2s, h2r, s0s, s0r, s1s, s1r, s2s, s2r, g2s, g2r, g1s, g1r, g0s, g0r, obs, obr,
+    x_ref, dy_ref, links_ref, local, h1s, h1r, h2s, h2r, s0s, s0r, s1s, s1r, s2s, s2r, g2s, g2r, g1s, g1r, g0s, g0r, obs, obr,
 ):
     batch = lax.axis_index("batch")
     at = lax.axis_index("space")
@@ -274,7 +274,8 @@
     loads = [
         pltpu.make_async_copy(src, dst, local.at[i])
         for i, (src, dst) in enumerate(
-            ((k1_hbm, k1_ref), (k2_hbm, k2_ref), (sq_hbm, sq_ref), (sr_hbm, sr_ref), (sc_hbm, sc_ref))
+            ((x_hbm, x_ref), (dy_hbm, dy_ref), (links_hbm, links_ref), (k1_hbm, k1_ref), (k2_hbm, k2_ref),
+             (sq_hbm, sq_ref), (sr_hbm, sr_ref), (sc_hbm, sc_ref))
         )
     ]
     for load in loads:
@@ -291,19 +292,17 @@
     lo = lane_ids(C) < 64
     zero = jnp.zeros((C, LANES), BF)
     mats = (sq_ref, sr_ref, sc_ref)
-    count = count_ref[0, 0]
+    for load in loads[:2]:
+        load.wait()
     for n in range(HOME):
         first_x, first_dy = x_ref[n, :, 0:LANES], dy_ref[n, :, 0:LANES]
         last_x, last_dy = x_ref[n, :, 3 * LANES :], dy_ref[n, :, 3 * LANES :]
         down1[n] = jnp.where(lo, swap_halves(last_x), last_dy)
         back1[n] = jnp.where(lo, first_dy, swap_halves(first_x))
-    pl.semaphore_wait(barrier, 28)
-    halo1 = exchange(down1, back1, low1, up1, h1s, h1r, space)
-    for copy in halo1:
-        copy.start()
-
     for tiles_ref, e0, e3 in ((xt, ex0, ex3), (yt, ey0, ey3), (ht, eh0, eh3), (gt, eg0, eg3)):
         clear_last(tiles_ref, e0, e3)
+    loads[2].wait()
+    count = count_ref[0, 0]
     for n in range(HOME):
         live = jnp.where(n < count, 1.0, 0.0).astype(F32)
         for src, tiles_ref, e0, e3 in ((x_ref, xt, ex0, ex3), (dy_ref, yt, ey0, ey3)):
@@ -313,13 +312,8 @@
                 tiles_ref[n, j] = tiles[j]
             e0[n] = swap_halves(tiles[0])
             e3[n] = swap_halves(tiles[3])
-    for ref in (gpad, hpad):
-        for j in (0, 1, 6, 7):
-            ref[j] = zero
     acc1[...] = jnp.zeros_like(acc1)
     acc2[...] = jnp.zeros_like(acc2)
-    for load in loads:
-        load.wait()
     field_x = (xt, ex0, ex3, lx, ux, dx)
     field_y = (yt, ey0, ey3, ly, uy, dd)
     field_h = (ht, eh0, eh3, lh, uh, dx)
@@ -329,17 +323,8 @@
         build_columns((field_x, field_y), INNER, links_ref, n, t_buf, mats)
         return 0
 
-    lax.fori_loop(0, HOME, first_inner, 0)
-    flip_kernels(k1_ref, k2_ref, f1_ref, f2_ref)
-    for copy in halo1:
-        copy.wait_recv()
-    unpack_halo(low1, up1, (lx, ly), (ux, uy))
-
-    def first_brick(n, _):
-        build_columns((field_x, field_y), EDGE, links_ref, n, t_buf, mats)
-        hidden = []
-        grads = []
-        for j in range(TILES):
+    def first_convs(n, tiles):
+        for j in tiles:
             pre = jnp.dot(
                 k1_ref[...], dx[n, j : j + 3].reshape(TAPS * C, LANES), preferred_element_type=F32
             )
@@ -347,20 +332,43 @@
                 f2_ref[...], dd[n, j : j + 3].reshape(TAPS * C, LANES), preferred_element_type=F32
             )
             sigma = 1.0 / (1.0 + jnp.exp(-pre))
-            hid = (pre * sigma).astype(BF)
-            gpre = (grad_hidden * (sigma * (1.0 + pre * (1.0 - sigma)))).astype(BF)
-            ht[n, j] = hid
-            gt[n, j] = gpre
-            hpad[j + 2] = hid
-            gpad[j + 2] = gpre
-            hidden.append(hid)
-            grads.append(gpre)
+            ht[n, j] = (pre * sigma).astype(BF)
+            gt[n, j] = (grad_hidden * (sigma * (1.0 + pre * (1.0 - sigma)))).astype(BF)
+
+    def first_middle(n, _):
+        first_convs(n, (1, 2))
+        return 0
+
+    for load in loads[5:]:
+        load.wait()
+    lax.fori_loop(0, WORK_CAP, first_inner, 0)
+    pl.semaphore_wait(barrier, 28)
+    halo1 = exchange(down1, back1, low1, up1, h1s, h1r, space)
+    for copy in halo1:
+        copy.start()
+    lax.fori_loop(WORK_CAP, HOME, first_inner, 0)
+    for load in loads[3:5]:
+        load.wait()
+    flip_kernels(k1_ref, k2_ref, f1_ref, f2_ref)
+    lax.fori_loop(0, HOME, first_middle, 0)
+    for copy in halo1:
+        copy.wait_recv()
+    unpack_halo(low1, up1, (lx, ly), (ux, uy))
+
+    def first_brick(n, _):
+        build_columns((field_x, field_y), EDGE, links_ref, n, t_buf, mats)
+        first_convs(n, (0, 3))
+        hidden = [ht[n, j] for j in range(TILES)]
+        grads = [gt[n, j] for j in range(TILES)]
         for tiles, e0, e3 in ((hidden, eh0, eh3), (grads, eg0, eg3)):
             e0[n] = swap_halves(tiles[0])
             e3[n] = swap_halves(tiles[3])
         down, back = halo_pack(hidden, grads, lo)
         down2[n] = down
         back2[n] = back
+        edges = [zero, zero]
+        hpad = edges + hidden + edges
+        gpad = edges + grads + edges
         for acc, cols, pad, flip in ((acc1, dx, gpad, False), (acc2, dd, hpad, True)):
             total = acc[...]
             for k in (0, 2, 4):
@@ -538,6 +546,10 @@
     return pltpu.VMEM(shape, BF)
 
 
+def in_place(*values):
+    return [pltpu.with_memory_space_constraint(v, pltpu.HBM) for v in values]
+
+
 def shards(space, groups, features, cotangent, brick_count, destination, neighbours, kernel_one, kernel_two):
     bricks_shape = jax.ShapeDtypeStruct((HOME, C, TILES * LANES), BF)
     sums_shape = jax.ShapeDtypeStruct((2, 16, C, LANES), BF)
@@ -545,7 +557,7 @@
     tiles = bf_scratch(HOME + 1, TILES, C, LANES)
     rows = bf_scratch(HOME + 1, C, LANES)
     field = [tiles] * 2 + [rows] * 8
-    anywhere = pl.BlockSpec(memory_space=pl.ANY)
+    anywhere = pl.BlockSpec(memory_space=pltpu.HBM)
     kernel_rows = bf_scratch(C, TAPS * C)
     out, grad_in, arrived, total = pl.pallas_call(
         functools.partial(block_kernel, space),
@@ -553,13 +565,12 @@
             bricks_shape, bricks_shape,
             jax.ShapeDtypeStruct((3, C, TILES * LANES), BF), sums_shape,
         ],
-        in_specs=[vmem()] * 2 + [smem()] * 2 + [anywhere] * 5,
+        in_specs=[anywhere] * 3 + [smem()] + [anywhere] * 5,
         out_specs=[vmem()] * 4,
         scratch_shapes=field
         + field
         + [bf_scratch(2 * TILES * C, 4 * LANES)]
         + [bf_scratch(HOME, SPAN, 9 * C, LANES)] * 2
-        + [bf_scratch(8, C, LANES)] * 2
         + [pltpu.VMEM((9 * C, 2 * LANES), F32)] * 2
         + [kernel_rows] * 2
         + [bf_scratch(2 * LANES, 2 * LANES)] * 2
@@ -577,12 +588,16 @@
             pltpu.VMEM((8, 8, LANES), F32),
             bf_scratch(C, LANES),
         ]
-        + [dma((5,))]
+        + [bf_scratch(HOME, C, TILES * LANES)] * 2
+        + [pltpu.SMEM((HOME, 1, 26), jnp.int32), dma((8,))]
         + [dma((n,)) for n in (2, 2, 1, 15, 7, 7, 15, 16, 3) for _ in range(2)],
         compiler_params=pltpu.CompilerParams(
             collective_id=0, has_side_effects=True, vmem_limit_bytes=VMEM_BYTES
         ),
-    )(features[0], cotangent[0], neighbours, brick_count, kernel_one, kernel_two, *shift_matrices())
+    )(
+        *in_place(features[0], cotangent[0], neighbours.transpose(2, 0, 1)), brick_count,
+        *in_place(kernel_one, kernel_two, *shift_matrices()),
+    )
     scale = 1.0 / math.sqrt(groups * space * HOME * TILES * LANES)
     grad_shape = jax.ShapeDtypeStruct((C, TAPS * C), F32)
     work, grad_out, grad_one, grad_two = pl.pallas_call(
@@ -594,7 +609,7 @@
         in_specs=[vmem()] * 4,
         out_specs=[vmem()] * 4,
         scratch_shapes=[pltpu.VMEM((2048, LANES), F32)],
-        compiler_params=pltpu.CompilerParams(vmem_limit_bytes=VMEM_BYTES),
+        compiler_params=pltpu.CompilerParams(vmem_limit_bytes=12 * 1024 * 1024),
     )(total, out, arrived, grad_in)
     return work[None], grad_out[None], grad_one, grad_two
 

time: 59.2 us -> 54.4 us (0.919)
  Pallas kernels: 57 us -> 53 us
  local copies, waits for them, and re-layouts: 0.71 us -> 0 us
    pallas_call x1, Pallas kernels: 54.3 us -> 51.5 us  [shards(): pl.pallas_call(functools.partial(block_kernel, space), out_shape=[bricks_...]
    pallas_call x1, Pallas kernels: 2.68 us -> 1.54 us  [shards(): pl.pallas_call(functools.partial(finish_kernel, scale), out_shape=[jax.Sh...]
    unnamed x3 -> x0, local copies, waits for them, and re-layouts: 0.71 us -> none
where the time goes in v4:
time: 54.4 us; the launch traced here: 54.3 us
  Pallas kernels  53 us (97%)
  between operations  1.29 us (2%)
    pallas_call x1, Pallas kernels, shards(): pl.pallas_call(functools.partial(block_kernel, space), out_shape=[bricks_...  51.5 us
    pallas_call x1, Pallas kernels, shards(): pl.pallas_call(functools.partial(finish_kernel, scale), out_shape=[jax.Sh...  1.54 us

profile of v4, /device:TPU:1, one launch (start us, length us, event | category | flops | bytes accessed | tf_op | source)
XLA Modules:
  0.0 54.3 jit_solution(14542712304841100430)
XLA Ops:
  1.3 51.5 %shard_map.120 = (bf16[5,64,512]{2,1,0:T(8,128)(2,1)S(1)}, bf16[5,64,512]{2,1,0:T(8,128)(2,1)S(1)}, bf16[3,64,512]{2,1,0:T(8,128)(2,1)S(1)}, bf16[2,16,64,128]{3,2,1,0:T(8,128)(2,1)S(1)}) custom-call(bf16[5,64,512]{2,1,0:T(8,128)(2,1)} %bitcast.5, bf16[5,64,512]{2,1,0:T(8,128)(2,1)} %bitcast.6, s32[5,1,26]{2,1,0:T(1,128)} %bitcast.7, ...), custom_call_target="tpu_custom_call" | custom-call | tf_op jit(solution)/shard_map/pallas_call | solution.py:562
  52.8 1.5 %shard_map.121 = (bf16[2,64,512]{2,1,0:T(8,128)(2,1)}, bf16[5,64,512]{2,1,0:T(8,128)(2,1)}, f32[64,1728]{1,0:T(8,128)}, f32[64,1728]{1,0:T(8,128)}) custom-call(bf16[2,16,64,128]{3,2,1,0:T(8,128)(2,1)S(1)} %get-tuple-element.12.total_ref, bf16[5,64,512]{2,1,0:T(8,128)(2,1)S(1)} %get-tuple-element.13.ob_ref, ...), custom_call_target="tpu_custom_call" | custom-call | tf_op jit(solution)/shard_map/pallas_call | solution.py:603

commit v5 on v4

--- a/solution.py
+++ b/solution.py
@@ -16,6 +16,7 @@
 C = 64
 LANES = 128
 TAPS = 27
+ROWS = 56
 VMEM_BYTES = 32 * 1024 * 1024
 MESH = pl.DeviceIdType.MESH
 BF = jnp.bfloat16
@@ -226,9 +227,9 @@
     ht, gt, eh0, eh3, eg0, eg3, lh, lg, uh, ug,
     t_buf, dx, dd, acc1, acc2,
     k1_ref, k2_ref, sq_ref, sr_ref, sc_ref, f1_ref, f2_ref,
-    down1, back1, down2, back2, low1, up1, low2, up2, sums32, sums16,
-    r0, s1, r1, p2, r2, q_buf, a2, chunk,
-    x_ref, dy_ref, links_ref, local, h1s, h1r, h2s, h2r, s0s, s0r, s1s, s1r, s2s, s2r, g2s, g2r, g1s, g1r, g0s, g0r, obs, obr,
+    down1, back1, down2, back2, low1, up1, low2, up2, flat, sums32,
+    r0, s1, r1, zbuf, rz, chunk,
+    x_ref, dy_ref, links_ref, local, h1s, h1r, h2s, h2r, s0s, s0r, s1s, s1r, g2s, g2r, g1s, g1r, g0s, g0r, obs, obr,
 ):
     batch = lax.axis_index("batch")
     at = lax.axis_index("space")
@@ -395,15 +396,13 @@
         jnp.where(wide, second_a, first_a),
         jnp.where(wide, first_a, second_a),
     )
-    for tap in range(2 * 16):
-        if tap < TAPS:
-            row = tap % 9 * C
-            value = parts[tap // 9][row : row + C]
-        else:
-            value = jnp.zeros((C, LANES), F32)
-        sums32[tap // 16, tap % 16] = value
-        sums16[tap // 16, tap % 16] = value.astype(BF)
-    pair = start(sums16.at[other], r0, s0s, s0r, 0, partner)
+    for i, part in enumerate(parts):
+        flat[i * 9 * C : (i + 1) * 9 * C, :] = part
+    flat[TAPS * C :, :] = jnp.zeros((32 * ROWS - TAPS * C, LANES), F32)
+    for i in range(32):
+        value = flat[i * ROWS : (i + 1) * ROWS, :]
+        sums32[i // 16, i % 16, 0:ROWS] = value
+    pair = start(sums32.at[other, :, 0:ROWS], r0.at[:, 0:ROWS], s0s, s0r, 0, partner)
     halo2 = exchange(down2, back2, low2, up2, h2s, h2r, space)
     for copy in halo2:
         copy.start()
@@ -416,9 +415,9 @@
     pair.wait_recv()
     for d in far_plane + [0]:
         place = plane_place(d)
-        s1[place] = (sums32[core, place] + r0[place].astype(F32)).astype(BF)
+        s1[place, 0:ROWS] = (sums32[core, place, 0:ROWS] + r0[place, 0:ROWS]).astype(BF)
     scatter = {
-        d: start(s1.at[plane_place(d)], r1.at[d - 1], s1s, s1r, d - 1, plane_peer(d))
+        d: start(s1.at[plane_place(d), 0:ROWS], r1.at[d - 1, 0:ROWS], s1s, s1r, d - 1, plane_peer(d))
         for d in far_plane
     }
     lax.fori_loop(WORK_CAP, HOME, second_inner, 0)
@@ -446,47 +445,45 @@
         return 0
 
     lax.fori_loop(WORK_CAP, HOME, second_brick, 0)
-    acc = s1[g].astype(F32)
+    acc = s1[g, 0:ROWS].astype(F32)
     for d in near_plane:
         scatter[d].wait_recv()
-        acc = acc + r1[d - 1].astype(F32)
-    p2[...] = acc.reshape(8, 8, LANES)
-    column_scatter = {
-        d: start(p2.at[column_place(d)], r2.at[d - 1], s2s, s2r, d - 1, column_peer(d))
+        acc = acc + r1[d - 1, 0:ROWS].astype(F32)
+    zbuf[0:ROWS] = acc.astype(BF)
+    rz[z, 0:ROWS] = acc.astype(BF)
+    column_gather = {
+        d: start(zbuf.at[0:ROWS], rz.at[z, 0:ROWS], g2s, g2r, d - 1, column_peer(d))
         for d in far_column
     }
     bricks = [
         start(out_ref.at[WORK_CAP + k], arrived.at[k], obs, obr, k, ring(k + 1)) for k in range(3)
     ]
     lax.fori_loop(0, WORK_CAP, second_brick, 0)
-    piece = p2[z]
-    for d in near_column:
-        column_scatter[d].wait_recv()
-        piece = piece + r2[d - 1]
-    q_buf[...] = piece
-    a2[z] = piece
-    column_gather = {
-        d: start(q_buf, a2.at[z], g2s, g2r, d - 1, column_peer(d)) for d in far_column
-    }
     for d in near_column:
         column_gather[d].wait_recv()
-    whole = a2[...].reshape(C, LANES).astype(BF)
-    chunk[...] = whole
-    total_ref[core, g] = whole
+    whole = rz[0, 0:ROWS].astype(F32)
+    for i in range(1, 8):
+        whole = whole + rz[i, 0:ROWS].astype(F32)
+    whole = whole.astype(BF)
+    chunk[0:ROWS] = whole
+    total_ref[core, g, 0:ROWS] = whole
+    used = chunk.at[0:ROWS]
     gather = {
-        d: start(chunk, total_ref.at[core, g], g1s, g1r, d - 1, plane_peer(d)) for d in far_plane
+        d: start(used, total_ref.at[core, g, 0:ROWS], g1s, g1r, d - 1, plane_peer(d)) for d in far_plane
     }
-    forward = [start(chunk, total_ref.at[core, g], g0s, g0r, 0, partner)]
+    forward = [start(used, total_ref.at[core, g, 0:ROWS], g0s, g0r, 0, partner)]
     for d in near_plane:
         gather[d].wait_recv()
         came = plane_place(d, -1)
         forward.append(
-            start(total_ref.at[core, came], total_ref.at[core, came], g0s, g0r, d, partner)
+            start(
+                total_ref.at[core, came, 0:ROWS], total_ref.at[core, came, 0:ROWS], g0s, g0r, d, partner
+            )
         )
     for copy in (*forward, *bricks):
         copy.wait_recv()
     for copy in (
-        *halo1, *halo2, pair, *scatter.values(), *column_scatter.values(),
+        *halo1, *halo2, pair, *scatter.values(),
         *column_gather.values(), *gather.values(), *forward, *bricks,
     ):
         copy.wait_send()
@@ -501,7 +498,8 @@
         arrived_ref[0].astype(F32) + arrived_ref[1].astype(F32) + arrived_ref[2].astype(F32)
     )
     work_ref[1] = (ob_ref[1].astype(F32) + extra).astype(BF)
-    total[...] = total_ref[...].reshape(2048, LANES).astype(F32) * scale
+    for i in range(32):
+        total[i * ROWS : (i + 1) * ROWS, :] = total_ref[i // 16, i % 16, 0:ROWS].astype(F32) * scale
     lo = lane_ids(C) < 64
 
     def block(tap):
@@ -577,20 +575,18 @@
         + [bf_scratch(4 * LANES, 4 * LANES)]
         + [kernel_rows] * 2
         + [bf_scratch(HOME, C, LANES)] * 8
-        + [pltpu.VMEM((2, 16, C, LANES), F32), bf_scratch(2, 16, C, LANES)]
+        + [pltpu.VMEM((32 * ROWS, LANES), F32)]
+        + [pltpu.VMEM((2, 16, C, LANES), F32), pltpu.VMEM((16, C, LANES), F32)]
         + [
             bf_scratch(16, C, LANES),
-            bf_scratch(16, C, LANES),
             bf_scratch(15, C, LANES),
-            pltpu.VMEM((8, 8, LANES), F32),
-            pltpu.VMEM((7, 8, LANES), F32),
-            pltpu.VMEM((8, LANES), F32),
-            pltpu.VMEM((8, 8, LANES), F32),
+            bf_scratch(C, LANES),
+            bf_scratch(8, C, LANES),
             bf_scratch(C, LANES),
         ]
         + [bf_scratch(HOME, C, TILES * LANES)] * 2
         + [pltpu.SMEM((HOME, 1, 26), jnp.int32), dma((8,))]
-        + [dma((n,)) for n in (2, 2, 1, 15, 7, 7, 15, 16, 3) for _ in range(2)],
+        + [dma((n,)) for n in (2, 2, 1, 15, 7, 15, 16, 3) for _ in range(2)],
         compiler_params=pltpu.CompilerParams(
             collective_id=0, has_side_effects=True, vmem_limit_bytes=VMEM_BYTES
         ),
@@ -608,7 +604,7 @@
         ],
         in_specs=[vmem()] * 4,
         out_specs=[vmem()] * 4,
-        scratch_shapes=[pltpu.VMEM((2048, LANES), F32)],
+        scratch_shapes=[pltpu.VMEM((32 * ROWS, LANES), F32)],
         compiler_params=pltpu.CompilerParams(vmem_limit_bytes=12 * 1024 * 1024),
     )(total, out, arrived, grad_in)
     return work[None], grad_out[None], grad_one, grad_two

time: 54.4 us -> 50.1 us (0.921)
  Pallas kernels: 53 us -> 48.7 us
    pallas_call x1, Pallas kernels: 51.5 us -> 47.2 us  [shards(): pl.pallas_call(functools.partial(block_kernel, space), out_shape=[bricks_...]
where the time goes in v5:
time: 50.1 us; the launch traced here: 50 us
  Pallas kernels  48.7 us (97%)
  between operations  1.29 us (3%)
    pallas_call x1, Pallas kernels, shards(): pl.pallas_call(functools.partial(block_kernel, space), out_shape=[bricks_...  47.2 us
    pallas_call x1, Pallas kernels, shards(): pl.pallas_call(functools.partial(finish_kernel, scale), out_shape=[jax.Sh...  1.54 us

profile of v5, /device:TPU:1, one launch (start us, length us, event | category | flops | bytes accessed | tf_op | source)
XLA Modules:
  0.0 50.0 jit_solution(6370735139930363607)
XLA Ops:
  1.3 47.2 %shard_map.120 = (bf16[5,64,512]{2,1,0:T(8,128)(2,1)S(1)}, bf16[5,64,512]{2,1,0:T(8,128)(2,1)S(1)}, bf16[3,64,512]{2,1,0:T(8,128)(2,1)S(1)}, bf16[2,16,64,128]{3,2,1,0:T(8,128)(2,1)S(1)}) custom-call(bf16[5,64,512]{2,1,0:T(8,128)(2,1)} %bitcast.5, bf16[5,64,512]{2,1,0:T(8,128)(2,1)} %bitcast.6, s32[5,1,26]{2,1,0:T(1,128)} %bitcast.7, ...), custom_call_target="tpu_custom_call" | custom-call | tf_op jit(solution)/shard_map/pallas_call | solution.py:560
  48.5 1.5 %shard_map.121 = (bf16[2,64,512]{2,1,0:T(8,128)(2,1)}, bf16[5,64,512]{2,1,0:T(8,128)(2,1)}, f32[64,1728]{1,0:T(8,128)}, f32[64,1728]{1,0:T(8,128)}) custom-call(bf16[2,16,64,128]{3,2,1,0:T(8,128)(2,1)S(1)} %get-tuple-element.12.total_ref, bf16[5,64,512]{2,1,0:T(8,128)(2,1)S(1)} %get-tuple-element.13.ob_ref, ...), custom_call_target="tpu_custom_call" | custom-call | tf_op jit(solution)/shard_map/pallas_call | solution.py:599

commit v6 on v5

--- a/solution.py
+++ b/solution.py
@@ -455,10 +455,10 @@
         d: start(zbuf.at[0:ROWS], rz.at[z, 0:ROWS], g2s, g2r, d - 1, column_peer(d))
         for d in far_column
     }
+    lax.fori_loop(0, WORK_CAP, second_brick, 0)
     bricks = [
         start(out_ref.at[WORK_CAP + k], arrived.at[k], obs, obr, k, ring(k + 1)) for k in range(3)
     ]
-    lax.fori_loop(0, WORK_CAP, second_brick, 0)
     for d in near_column:
         column_gather[d].wait_recv()
     whole = rz[0, 0:ROWS].astype(F32)

time: 50.1 us -> 49.8 us (level)
  no operation moved by 1% of the time
where the time goes in v6:
time: 49.8 us; the launch traced here: 49.7 us
  Pallas kernels  48.4 us (97%)
  between operations  1.29 us (3%)
    pallas_call x1, Pallas kernels, shards(): pl.pallas_call(functools.partial(block_kernel, space), out_shape=[bricks_...  46.9 us
    pallas_call x1, Pallas kernels, shards(): pl.pallas_call(functools.partial(finish_kernel, scale), out_shape=[jax.Sh...  1.54 us

profile of v6, /device:TPU:1, one launch (start us, length us, event | category | flops | bytes accessed | tf_op | source)
XLA Modules:
  0.0 49.7 jit_solution(10345681419724131597)
XLA Ops:
  1.3 46.9 %shard_map.120 = (bf16[5,64,512]{2,1,0:T(8,128)(2,1)S(1)}, bf16[5,64,512]{2,1,0:T(8,128)(2,1)S(1)}, bf16[3,64,512]{2,1,0:T(8,128)(2,1)S(1)}, bf16[2,16,64,128]{3,2,1,0:T(8,128)(2,1)S(1)}) custom-call(bf16[5,64,512]{2,1,0:T(8,128)(2,1)} %bitcast.5, bf16[5,64,512]{2,1,0:T(8,128)(2,1)} %bitcast.6, s32[5,1,26]{2,1,0:T(1,128)} %bitcast.7, ...), custom_call_target="tpu_custom_call" | custom-call | tf_op jit(solution)/shard_map/pallas_call | solution.py:560
  48.2 1.5 %shard_map.121 = (bf16[2,64,512]{2,1,0:T(8,128)(2,1)}, bf16[5,64,512]{2,1,0:T(8,128)(2,1)}, f32[64,1728]{1,0:T(8,128)}, f32[64,1728]{1,0:T(8,128)}) custom-call(bf16[2,16,64,128]{3,2,1,0:T(8,128)(2,1)S(1)} %get-tuple-element.12.total_ref, bf16[5,64,512]{2,1,0:T(8,128)(2,1)S(1)} %get-tuple-element.13.ob_ref, ...), custom_call_target="tpu_custom_call" | custom-call | tf_op jit(solution)/shard_map/pallas_call | solution.py:599
